TPU v7x, 32 devices: a whole 2x2x4 slice. The times are simulated.
32 devices in a mesh: tm: 8 (over z, y), space: 4 (over x, core).
Axes of the slice: x: 2, y: 2, z: 4, core: 2. Of those that a mesh axis runs over, the one named last changes fastest.
Arguments:
- start_values: float32 [8, 2, 1024, 1024], P('tm', None, 'space'), may hold values from -6 to 6
- node_values: float32 [8, 2, 2, 1024, 1024], P('tm', None, None, 'space'), may hold values from -6 to 6
Outputs:
- next_start: float32 [8, 2, 1024, 1024], P('tm', None, 'space')
- next_nodes: float32 [8, 2, 2, 1024, 1024], P('tm', None, None, 'space')
All inputs are finite; a program needn't handle non-finite values.
Results may differ from a plain program's by a relative error of at most 0.00002.
Values sent between devices are 32-bit elements; how exact they have to be, the bound alone decides.
A program may use at most 64 MiB of HBM per device.

v0:
```python
import jax
import jax.numpy as jnp
from jax import lax
from jax.experimental import pallas as pl
from jax.experimental.pallas import tpu as pltpu
from jax.sharding import PartitionSpec as P

CX = 256

diffusion = 1.5
drift = 0.8
shear = 0.6
first_weights = (5.0 / 24.0, 1.0 / 3.0, -1.0 / 24.0)
second_weights = (-1.0 / 24.0, 1.0 / 3.0, 5.0 / 24.0)
whole_weights = (1.0 / 6.0, 2.0 / 3.0, 1.0 / 6.0)

MESH = pl.DeviceIdType.MESH
HALO = 8
BLOCK = 32
PARTS = 4
STRIPS = 2
WHOLES = 1
LANES = 128


def weighted(weights, fields):
    return [sum(w * f[k] for w, f in zip(weights, fields)) for k in range(2)]


def times(real, imag, field):
    return [real * field[0] - imag * field[1], real * field[1] + imag * field[0]]


def coupled(factor, field):
    length = field[0].shape[0]
    sums = [pltpu.roll(f, 1, 0) + pltpu.roll(f, length - 1, 0) for f in field]
    return [factor * sums[1], -factor * sums[0]]


def kernel(
    begin_hbm,
    nodes_hbm,
    start_out,
    nodes_out,
    ext,
    gain,
    shift,
    load_sem,
    start_sem,
    halo_send,
    halo_recv,
    bulk_send,
    bulk_recv,
    relay_send,
    relay_recv,
):
    slab, columns = begin_hbm.shape[1:]
    peers, count = lax.axis_size("space"), lax.axis_size("tm")
    total = slab * peers
    tm, rank = lax.axis_index("tm"), lax.axis_index("space")
    has_prev, has_next = tm > 0, tm < count - 1
    has_up, has_down = rank > 0, rank < peers - 1
    blocks = slab // BLOCK
    low_row = total // 2 - CX // 2
    low_column = columns // 2 - CX // 2
    coarse_rows = gain.shape[1]
    coarse_blocks = coarse_rows // BLOCK
    coarse_rank = (rank * slab < low_row + CX) & (rank * slab + slab > low_row)
    lower = rank < peers // 2
    coarse_start = jnp.clip(low_row - rank * slab, 0, slab - coarse_rows)
    coarse_block = coarse_start // BLOCK
    first = jnp.where(
        coarse_rank,
        jnp.where(lower, coarse_block, blocks - coarse_block - coarse_blocks),
        0,
    )

    def mirrored(index):
        return jnp.where(lower, index, blocks - 1 - index)

    def block_of(step):
        return mirrored(jnp.where(step < blocks - first, first + step, blocks - 1 - step))

    def load_of(step):
        later = jnp.where(step <= blocks - first, first + step - 1, blocks - 1 - step)
        early = jnp.where(step == 2, first - 1, first + step)
        moved = jnp.where(step <= 2, early, later)
        return mirrored(jnp.where(first == 0, step, moved))

    def rows_of(block):
        return pl.ds(pl.multiple_of(block * BLOCK, BLOCK), BLOCK)

    def loads(step):
        block = load_of(step)
        source = rows_of(block)
        target = pl.ds(pl.multiple_of(block * BLOCK + HALO, HALO), BLOCK)
        return (
            pltpu.make_async_copy(
                begin_hbm.at[:, source, :], ext.at[0, :, target, :], load_sem.at[0, step]
            ),
            pltpu.make_async_copy(
                nodes_hbm.at[:, :, source, :],
                ext.at[1:3, :, target, :],
                load_sem.at[1, step],
            ),
        )

    def halos(side):
        source = pl.ds(0 if side == 0 else slab - HALO, HALO)
        target = pl.ds(slab + HALO if side == 0 else 0, HALO)
        there = {"space": rank - 1 if side == 0 else rank + 1}
        return (
            pltpu.make_async_remote_copy(
                begin_hbm.at[:, source, :],
                ext.at[0, :, target, :],
                halo_send.at[0, side],
                halo_recv.at[0, side],
                device_id=there,
                device_id_type=MESH,
            ),
            pltpu.make_async_remote_copy(
                nodes_hbm.at[:, :, source, :],
                ext.at[1:3, :, target, :],
                halo_send.at[1, side],
                halo_recv.at[1, side],
                device_id=there,
                device_id_type=MESH,
            ),
        )

    following = {"tm": tm + 1}

    def relay_copy(step):
        place = (slice(None), rows_of(block_of(step)), pl.ds(low_column, CX))
        return pltpu.make_async_remote_copy(
            nodes_out.at[(1,) + place],
            start_out.at[place],
            relay_send.at[step],
            relay_recv.at[step],
            device_id=following,
            device_id_type=MESH,
        )

    def bulk(unit, act):
        step, part = unit // PARTS, unit % PARTS
        block = block_of(step)
        strip = coarse_rank & (step < coarse_blocks)

        def copy(place):
            return pltpu.make_async_remote_copy(
                nodes_out.at[(1,) + place],
                start_out.at[place],
                bulk_send.at[unit],
                bulk_recv.at[unit],
                device_id=following,
                device_id_type=MESH,
            )

        @pl.when(strip & (part >= PARTS - STRIPS))
        def _():
            height = 2 * BLOCK // STRIPS
            top = pl.multiple_of(block * BLOCK + (part - (PARTS - STRIPS)) // 2 * height, HALO)
            left = pl.multiple_of((part % 2) * (low_column + CX), LANES)
            act(copy((slice(None), pl.ds(top, height), pl.ds(left, low_column))))

        quick = (step == 0) & jnp.logical_not(coarse_rank)

        @pl.when(quick)
        def _():
            width = columns // PARTS
            left = pl.multiple_of(part * width, LANES)
            act(copy((slice(None), rows_of(block), pl.ds(left, width))))

        @pl.when(jnp.logical_not(quick | strip) & ((part + 1) % (PARTS // WHOLES) == 0))
        def _():
            width = columns // WHOLES
            left = pl.multiple_of(part // (PARTS // WHOLES) * width, LANES)
            act(copy((slice(None), rows_of(block), pl.ds(left, width))))

    def send(low, high):
        @pl.when(has_next)
        def _():
            @pl.loop(low, high)
            def _(unit):
                bulk(unit, lambda c: c.start())

    whole_start = pltpu.make_async_copy(begin_hbm, start_out, start_sem)

    barrier = pltpu.get_barrier_semaphore()
    for there, exists in (
        ({"space": rank - 1}, has_up),
        ({"space": rank + 1}, has_down),
        ({"tm": tm - 1}, has_prev),
        ({"tm": tm + 1}, has_next),
    ):

        @pl.when(exists)
        def _(there=there):
            pl.semaphore_signal(barrier, inc=1, device_id=there, device_id_type=MESH)

    @pl.loop(0, blocks)
    def _(step):
        for c in loads(step):
            c.start()

    for side, exists in ((0, has_up), (1, has_down)):

        @pl.when(jnp.logical_not(exists))
        def _(side=side):
            edge = pl.ds(0 if side == 0 else slab + HALO, HALO)
            ext[:, :, edge, :] = jnp.zeros((3, 2, HALO, columns), jnp.float32)

    @pl.when(jnp.logical_not(has_prev))
    def _():
        whole_start.start()

    def greet():
        friends = sum(jnp.where(e, 1, 0) for e in (has_up, has_down, has_prev, has_next))
        pl.semaphore_wait(barrier, friends)
        for side, exists in ((0, has_up), (1, has_down)):

            @pl.when(exists)
            def _(side=side):
                for c in halos(side):
                    c.start()

    def strip_compute(block, column, coarse):
        length = BLOCK + 2 * HALO
        span = pl.ds(pl.multiple_of(block * BLOCK, BLOCK), length)
        here = pl.ds(column, LANES)
        begin, one, two = [[ext[f, k, span, here] for k in range(2)] for f in range(3)]
        row = lax.broadcasted_iota(jnp.int32, (length, LANES), 0)
        row = row + (rank * slab + block * BLOCK - HALO)
        along = (row - total // 2).astype(jnp.float32) / (total // 2)
        place = lax.broadcasted_iota(jnp.int32, (1, LANES), 1) + column
        across = (place - columns // 2).astype(jnp.float32) / (columns // 2)
        inside = jnp.where((row >= 0) & (row < total), 1.0, 0.0).astype(jnp.float32)
        real = -diffusion * (along * along + across * across)
        imag = -drift * across
        factor = shear * across
        half_real, half_imag = 1.0 - 0.5 * real, -0.5 * imag
        scale = 1.0 / (half_real * half_real + half_imag * half_imag)
        inverse = (half_real * scale, -half_imag * scale)
        sum_one = weighted(first_weights, (begin, one, two))
        sum_two = weighted(second_weights, (begin, one, two))
        moved = times(real, imag, [s - 0.5 * o for s, o in zip(sum_one, one)])
        turned = coupled(factor, sum_one)
        inner = [begin[k] + moved[k] + turned[k] for k in range(2)]
        node_one = [inside * f for f in times(*inverse, inner)]
        moved = times(real, imag, [s - 0.5 * o for s, o in zip(sum_two, two)])
        turned = coupled(
            factor, [sum_two[k] + 0.5 * (node_one[k] - one[k]) for k in range(2)]
        )
        inner = [node_one[k] + moved[k] + turned[k] for k in range(2)]
        node_two = times(*inverse, inner)
        own = slice(HALO, HALO + BLOCK)
        rows = rows_of(block)
        if not coarse:
            for k in range(2):
                nodes_out[0, k, rows, here] = node_one[k][own]
                nodes_out[1, k, rows, here] = node_two[k][own]
            return
        mean = weighted(whole_weights, (begin, node_one, node_two))
        moved = times(real, imag, [mean[k] - node_two[k] for k in range(2)])
        turned = coupled(factor, mean)
        offset = [moved[k] + turned[k] for k in range(2)]
        step_real, step_imag = 1.0 - real, -imag
        scale = 1.0 / (step_real * step_real + step_imag * step_imag)
        grown = (step_real * scale, -step_imag * scale)
        offset = times(*grown, offset)
        local = pl.ds(pl.multiple_of(block * BLOCK - coarse_start, BLOCK), BLOCK)
        inner_here = pl.ds(pl.multiple_of(column - low_column, LANES), LANES)
        for k in range(2):
            gain[k, local, inner_here] = grown[k][own]
            shift[k, local, inner_here] = offset[k][own]
            kept = node_one[k] - 0.5 * (begin[k] + node_two[k])
            nodes_out[0, k, rows, here] = kept[own]

    lead = jnp.where(first == 0, 2, 3)

    def compute(step, after=None):
        block = block_of(step)
        arrived = jnp.where(step == 0, 0, step + lead - 1)

        @pl.loop(arrived, jnp.minimum(step + lead, blocks))
        def _(which):
            for c in loads(which):
                c.wait()

        @pl.when((block == blocks - 1) & has_down)
        def _():
            for c in halos(0):
                c.wait_recv()

        @pl.when((block == 0) & has_up)
        def _():
            for c in halos(1):
                c.wait_recv()

        in_coarse = coarse_rank & (step < coarse_blocks)
        strips = columns // LANES // PARTS

        @pl.loop(0, PARTS)
        def _(part):
            @pl.loop(0, strips)
            def _(index):
                low = (part * strips + index) * LANES
                column = pl.multiple_of(low, LANES)
                if after is not None:
                    strip_compute(block, column, False)
                    return
                coarse = in_coarse & (low >= low_column) & (low < low_column + CX)

                @pl.when(coarse)
                def _():
                    strip_compute(block, column, True)

                @pl.when(jnp.logical_not(coarse))
                def _():
                    strip_compute(block, column, False)

            if after is not None:
                after(PARTS * step + part)

    def relay():
        @pl.when(jnp.logical_not(has_prev))
        def _():
            whole_start.wait()

        @pl.loop(0, coarse_blocks)
        def _(step):
            @pl.when(has_prev)
            def _():
                relay_copy(step).wait_recv()

            block = block_of(step)
            rows = rows_of(block)
            local = pl.ds(pl.multiple_of(block * BLOCK - coarse_start, BLOCK), BLOCK)
            here = pl.ds(low_column, CX)
            begin = [start_out[k, rows, here] for k in range(2)]
            grown = times(gain[0, local, :], gain[1, local, :], begin)
            finish = [grown[k] + shift[k, local, :] for k in range(2)]
            for k in range(2):
                nodes_out[1, k, rows, here] = finish[k]

            @pl.when(has_next)
            def _():
                relay_copy(step).start()

            for k in range(2):
                nodes_out[0, k, rows, here] += 0.5 * (begin[k] + finish[k])

    units = PARTS * blocks
    waiting = jnp.minimum(PARTS * tm // 2, units)
    opening = jnp.where(has_prev, jnp.minimum(waiting, PARTS * coarse_blocks), PARTS * coarse_blocks)
    middle = jnp.maximum(waiting, opening)

    @pl.when(coarse_rank)
    def _():
        greet()

        @pl.loop(0, coarse_blocks)
        def _(step):
            compute(step)

        @pl.when(jnp.logical_not(has_prev))
        def _():
            relay()

        send(0, opening)

        @pl.loop(coarse_blocks, blocks)
        def _(step):
            compute(step)

        send(opening, middle)

        @pl.when(has_prev)
        def _():
            relay()

        send(middle, units)

    @pl.when(jnp.logical_not(coarse_rank))
    def _():
        def after(unit):
            @pl.when(unit == 0)
            def _():
                greet()

            send(unit, unit + 1)

        @pl.loop(0, blocks)
        def _(step):
            compute(step, after)

        @pl.when(jnp.logical_not(has_prev))
        def _():
            whole_start.wait()

    for side, exists in ((0, has_up), (1, has_down)):

        @pl.when(exists)
        def _(side=side):
            for c in halos(side):
                c.wait_send()

    @pl.when(coarse_rank & has_next)
    def _():
        @pl.loop(0, coarse_blocks)
        def _(step):
            relay_copy(step).wait_send()

    @pl.when(has_prev)
    def _():
        @pl.loop(0, units)
        def _(unit):
            bulk(unit, lambda c: c.wait_recv())

    @pl.when(has_next)
    def _():
        @pl.loop(0, units)
        def _(unit):
            bulk(unit, lambda c: c.wait_send())


def write_out(start, nodes, start_hbm, nodes_hbm, sem):
    copies = [
        pltpu.make_async_copy(nodes.at[f, k], nodes_hbm.at[f, k], sem.at[2 * f + k])
        for f in range(2)
        for k in range(2)
    ]
    copies += [pltpu.make_async_copy(start.at[k], start_hbm.at[k], sem.at[4 + k]) for k in range(2)]
    for c in copies:
        c.start()
    for c in copies:
        c.wait()


def body(start_values, node_values):
    slab, columns = start_values.shape[2:]
    peers = lax.axis_size("space")
    coarse_rows = min(slab, max(CX // 2, CX // peers))
    blocks, coarse_blocks = slab // BLOCK, coarse_rows // BLOCK
    hbm = pl.BlockSpec(memory_space=pltpu.HBM)
    vmem = pl.BlockSpec(memory_space=pltpu.VMEM)
    dma = pltpu.SemaphoreType.DMA
    start, nodes = pl.pallas_call(
        kernel,
        out_shape=(
            OUT((2, slab, columns), jnp.float32),
            OUT((2, 2, slab, columns), jnp.float32),
        ),
        in_specs=[hbm, hbm],
        out_specs=(vmem, vmem),
        scratch_shapes=[
            pltpu.VMEM((3, 2, slab + 2 * HALO, columns), jnp.float32),
            pltpu.VMEM((2, coarse_rows, CX), jnp.float32),
            pltpu.VMEM((2, coarse_rows, CX), jnp.float32),
            dma((2, blocks)),
            dma,
            dma((2, 2)),
            dma((2, 2)),
            dma((PARTS * blocks,)),
            dma((PARTS * blocks,)),
            dma((coarse_blocks,)),
            dma((coarse_blocks,)),
        ],
        compiler_params=pltpu.CompilerParams(
            collective_id=0, has_side_effects=True, vmem_limit_bytes=56 * 1024 * 1024
        ),
    )(start_values[0], node_values[0])
    start, nodes = pl.pallas_call(
        write_out,
        out_shape=(
            jax.ShapeDtypeStruct(start.shape, jnp.float32),
            jax.ShapeDtypeStruct(nodes.shape, jnp.float32),
        ),
        in_specs=[pl.BlockSpec(memory_space=pl.ANY)] * 2,
        out_specs=(hbm, hbm),
        scratch_shapes=[dma((6,))],
        compiler_params=pltpu.CompilerParams(vmem_limit_bytes=2 * 1024 * 1024),
    )(start, nodes)
    return (start[None], nodes[None])


OUT = pltpu.VMEM


def solution(mesh):
    in_specs = (P("tm", None, "space", None), P("tm", None, None, "space", None))
    out_specs = (P("tm", None, "space", None), P("tm", None, None, "space", None))
    return jax.shard_map(body, mesh=mesh, in_specs=in_specs, out_specs=out_specs, check_vma=False)
```

profile of v0, /device:TPU:9, one launch (start us, length us, event | category | flops | bytes accessed | tf_op | source)
XLA Modules:
  0.0 54.0 jit_solution(6222111837623256092)
XLA Ops:
  0.6 50.7 %shard_map.41 = (f32[2,256,1024]{2,1,0:T(8,128)S(1)}, f32[2,2,256,1024]{3,2,1,0:T(8,128)S(1)}) custom-call(f32[2,256,1024]{2,1,0:T(8,128)} %bitcast.5, f32[2,2,256,1024]{3,2,1,0:T(8,128)} %bitcast.4), custom_call_target="tpu_custom_call" | custom-call | tf_op jit(solution)/shard_map/pallas_call | solution.py:448
  51.3 2.7 %shard_map.42 = (f32[2,256,1024]{2,1,0:T(8,128)}, f32[2,2,256,1024]{3,2,1,0:T(8,128)}) custom-call(f32[2,256,1024]{2,1,0:T(8,128)S(1)} %get-tuple-element.6.start, f32[2,2,256,1024]{3,2,1,0:T(8,128)S(1)} %get-tuple-element.7.nodes), custom_call_target="tpu_custom_call" | custom-call | tf_op jit(solution)/shard_map/pallas_call | solution.py:473
where the time goes:
time: 54.2 us; the launch traced here: 54 us
  Pallas kernels  53.4 us (99%)
  between operations  0.64 us (1%)
    pallas_call x1, Pallas kernels, body(): pl.pallas_call(kernel, out_shape=(OUT((2, slab, columns), jnp.float32), O...  50.7 us
    pallas_call x1, Pallas kernels, body(): pl.pallas_call(write_out, out_shape=(jax.ShapeDtypeStruct(start.shape, jn...  2.72 us

commit v1 on v0

--- a/solution.py
+++ b/solution.py
@@ -18,8 +18,7 @@
 HALO = 8
 BLOCK = 32
 PARTS = 4
-STRIPS = 2
-WHOLES = 1
+TURN = 3
 LANES = 128
 
 
@@ -65,6 +64,7 @@
     low_column = columns // 2 - CX // 2
     coarse_rows = gain.shape[1]
     coarse_blocks = coarse_rows // BLOCK
+    inward = min(HALO, slab - coarse_rows)
     coarse_rank = (rank * slab < low_row + CX) & (rank * slab + slab > low_row)
     lower = rank < peers // 2
     coarse_start = jnp.clip(low_row - rank * slab, 0, slab - coarse_rows)
@@ -74,36 +74,71 @@
         jnp.where(lower, coarse_block, blocks - coarse_block - coarse_blocks),
         0,
     )
-
-    def mirrored(index):
+    ascending = lower != coarse_rank
+
+    def block_of(step):
+        index = jnp.where(step < blocks - first, first + step, blocks - 1 - step)
         return jnp.where(lower, index, blocks - 1 - index)
-
-    def block_of(step):
-        return mirrored(jnp.where(step < blocks - first, first + step, blocks - 1 - step))
-
-    def load_of(step):
-        later = jnp.where(step <= blocks - first, first + step - 1, blocks - 1 - step)
-        early = jnp.where(step == 2, first - 1, first + step)
-        moved = jnp.where(step <= 2, early, later)
-        return mirrored(jnp.where(first == 0, step, moved))
 
     def rows_of(block):
         return pl.ds(pl.multiple_of(block * BLOCK, BLOCK), BLOCK)
 
-    def loads(step):
-        block = load_of(step)
-        source = rows_of(block)
-        target = pl.ds(pl.multiple_of(block * BLOCK + HALO, HALO), BLOCK)
-        return (
+    def load(slot, top, height, left, width, act):
+        top, left = pl.multiple_of(top, HALO), pl.multiple_of(left, LANES)
+        source, here = pl.ds(top, height), pl.ds(left, width)
+        target = pl.ds(pl.multiple_of(top + HALO, HALO), height)
+        act(
             pltpu.make_async_copy(
-                begin_hbm.at[:, source, :], ext.at[0, :, target, :], load_sem.at[0, step]
-            ),
+                begin_hbm.at[:, source, here], ext.at[0, :, target, here], load_sem.at[0, slot]
+            )
+        )
+        act(
             pltpu.make_async_copy(
-                nodes_hbm.at[:, :, source, :],
-                ext.at[1:3, :, target, :],
-                load_sem.at[1, step],
-            ),
+                nodes_hbm.at[:, :, source, here],
+                ext.at[1:3, :, target, here],
+                load_sem.at[1, slot],
+            )
         )
+
+    def load_step(step, act):
+        @pl.when(step < blocks - 1)
+        def _():
+            top = block_of(step) * BLOCK + jnp.where(ascending, HALO, -HALO)
+            load(PARTS + step, top, BLOCK, 0, columns, act)
+
+        @pl.when(step == blocks - 1)
+        def _():
+            height = BLOCK - HALO
+            load(PARTS + step, jnp.where(ascending, slab - height, 0), height, 0, columns, act)
+
+    def load_part(part, act):
+        height, width = BLOCK + HALO, columns // PARTS
+        load(part, jnp.where(ascending, 0, slab - height), height, part * width, width, act)
+
+    def load_coarse(slot, act):
+        height = coarse_rows + inward
+        top = jnp.where(lower, slab - height, 0)
+        if slot == 0:
+            load(0, top, height, low_column, CX, act)
+        else:
+            load(slot, top, height, (slot - 1) * (low_column + CX), low_column, act)
+
+    def begin_copies(act):
+        def copy(index, top, height, left, width):
+            place = (slice(None), pl.ds(pl.multiple_of(top, HALO), height), pl.ds(left, width))
+            act(pltpu.make_async_copy(begin_hbm.at[place], start_out.at[place], start_sem.at[index]))
+
+        @pl.when(coarse_rank)
+        def _():
+            copy(0, coarse_start, coarse_rows, 0, low_column)
+            copy(1, coarse_start, coarse_rows, low_column + CX, low_column)
+            if slab > coarse_rows:
+                top = jnp.where(lower, 0, coarse_rows)
+                copy(2, top, slab - coarse_rows, 0, columns)
+
+        @pl.when(jnp.logical_not(coarse_rank))
+        def _():
+            copy(0, 0, slab, 0, columns)
 
     def halos(side):
         source = pl.ds(0 if side == 0 else slab - HALO, HALO)
@@ -146,36 +181,32 @@
         block = block_of(step)
         strip = coarse_rank & (step < coarse_blocks)
 
-        def copy(place):
-            return pltpu.make_async_remote_copy(
-                nodes_out.at[(1,) + place],
-                start_out.at[place],
-                bulk_send.at[unit],
-                bulk_recv.at[unit],
-                device_id=following,
-                device_id_type=MESH,
+        def copy(left, width):
+            place = (slice(None), rows_of(block), pl.ds(pl.multiple_of(left, LANES), width))
+            act(
+                pltpu.make_async_remote_copy(
+                    nodes_out.at[(1,) + place],
+                    start_out.at[place],
+                    bulk_send.at[unit],
+                    bulk_recv.at[unit],
+                    device_id=following,
+                    device_id_type=MESH,
+                )
             )
 
-        @pl.when(strip & (part >= PARTS - STRIPS))
-        def _():
-            height = 2 * BLOCK // STRIPS
-            top = pl.multiple_of(block * BLOCK + (part - (PARTS - STRIPS)) // 2 * height, HALO)
-            left = pl.multiple_of((part % 2) * (low_column + CX), LANES)
-            act(copy((slice(None), pl.ds(top, height), pl.ds(left, low_column))))
+        @pl.when(strip & (part >= PARTS - 2))
+        def _():
+            copy((part - (PARTS - 2)) * (low_column + CX), low_column)
 
         quick = (step == 0) & jnp.logical_not(coarse_rank)
 
         @pl.when(quick)
         def _():
-            width = columns // PARTS
-            left = pl.multiple_of(part * width, LANES)
-            act(copy((slice(None), rows_of(block), pl.ds(left, width))))
-
-        @pl.when(jnp.logical_not(quick | strip) & ((part + 1) % (PARTS // WHOLES) == 0))
-        def _():
-            width = columns // WHOLES
-            left = pl.multiple_of(part // (PARTS // WHOLES) * width, LANES)
-            act(copy((slice(None), rows_of(block), pl.ds(left, width))))
+            copy(part * (columns // PARTS), columns // PARTS)
+
+        @pl.when(jnp.logical_not(quick | strip) & (part == PARTS - 1))
+        def _():
+            copy(0, columns)
 
     def send(low, high):
         @pl.when(has_next)
@@ -183,8 +214,6 @@
             @pl.loop(low, high)
             def _(unit):
                 bulk(unit, lambda c: c.start())
-
-    whole_start = pltpu.make_async_copy(begin_hbm, start_out, start_sem)
 
     barrier = pltpu.get_barrier_semaphore()
     for there, exists in (
@@ -198,10 +227,26 @@
         def _(there=there):
             pl.semaphore_signal(barrier, inc=1, device_id=there, device_id_type=MESH)
 
-    @pl.loop(0, blocks)
+    def start(copy):
+        copy.start()
+
+    def wait(copy):
+        copy.wait()
+
+    @pl.when(coarse_rank)
+    def _():
+        for slot in range(3):
+            load_coarse(slot, start)
+
+    @pl.when(jnp.logical_not(coarse_rank))
+    def _():
+        @pl.loop(0, PARTS)
+        def _(part):
+            load_part(part, start)
+
+    @pl.loop(jnp.where(coarse_rank, coarse_blocks, 1), blocks)
     def _(step):
-        for c in loads(step):
-            c.start()
+        load_step(step, start)
 
     for side, exists in ((0, has_up), (1, has_down)):
 
@@ -212,7 +257,7 @@
 
     @pl.when(jnp.logical_not(has_prev))
     def _():
-        whole_start.start()
+        begin_copies(start)
 
     def greet():
         friends = sum(jnp.where(e, 1, 0) for e in (has_up, has_down, has_prev, has_next))
@@ -223,6 +268,14 @@
             def _(side=side):
                 for c in halos(side):
                     c.start()
+
+    def halo_wait(block):
+        for side, edge in ((0, (block == blocks - 1) & has_down), (1, (block == 0) & has_up)):
+
+            @pl.when(edge)
+            def _(side=side):
+                for c in halos(side):
+                    c.wait_recv()
 
     def strip_compute(block, column, coarse):
         length = BLOCK + 2 * HALO
@@ -276,58 +329,21 @@
             kept = node_one[k] - 0.5 * (begin[k] + node_two[k])
             nodes_out[0, k, rows, here] = kept[own]
 
-    lead = jnp.where(first == 0, 2, 3)
-
-    def compute(step, after=None):
+        @pl.when(jnp.logical_not(has_prev))
+        def _():
+            for k in range(2):
+                start_out[k, rows, here] = begin[k][own]
+
+    def coarse_compute(step):
         block = block_of(step)
-        arrived = jnp.where(step == 0, 0, step + lead - 1)
-
-        @pl.loop(arrived, jnp.minimum(step + lead, blocks))
-        def _(which):
-            for c in loads(which):
-                c.wait()
-
-        @pl.when((block == blocks - 1) & has_down)
-        def _():
-            for c in halos(0):
-                c.wait_recv()
-
-        @pl.when((block == 0) & has_up)
-        def _():
-            for c in halos(1):
-                c.wait_recv()
-
-        in_coarse = coarse_rank & (step < coarse_blocks)
-        strips = columns // LANES // PARTS
-
-        @pl.loop(0, PARTS)
-        def _(part):
-            @pl.loop(0, strips)
-            def _(index):
-                low = (part * strips + index) * LANES
-                column = pl.multiple_of(low, LANES)
-                if after is not None:
-                    strip_compute(block, column, False)
-                    return
-                coarse = in_coarse & (low >= low_column) & (low < low_column + CX)
-
-                @pl.when(coarse)
-                def _():
-                    strip_compute(block, column, True)
-
-                @pl.when(jnp.logical_not(coarse))
-                def _():
-                    strip_compute(block, column, False)
-
-            if after is not None:
-                after(PARTS * step + part)
-
-    def relay():
-        @pl.when(jnp.logical_not(has_prev))
-        def _():
-            whole_start.wait()
-
-        @pl.loop(0, coarse_blocks)
+        halo_wait(block)
+
+        @pl.loop(0, CX // LANES)
+        def _(index):
+            strip_compute(block, pl.multiple_of(low_column + index * LANES, LANES), True)
+
+    def relay(low, high):
+        @pl.loop(low, high)
         def _(step):
             @pl.when(has_prev)
             def _():
@@ -351,52 +367,80 @@
                 nodes_out[0, k, rows, here] += 0.5 * (begin[k] + finish[k])
 
     units = PARTS * blocks
-    waiting = jnp.minimum(PARTS * tm // 2, units)
-    opening = jnp.where(has_prev, jnp.minimum(waiting, PARTS * coarse_blocks), PARTS * coarse_blocks)
-    middle = jnp.maximum(waiting, opening)
+    never = blocks + 1
+    turn = jnp.where(coarse_rank, jnp.minimum(TURN * tm, blocks), never)
+    early = jnp.where(coarse_rank, jnp.minimum(tm // 2, turn), blocks)
 
     @pl.when(coarse_rank)
     def _():
         greet()
-
-        @pl.loop(0, coarse_blocks)
+        load_coarse(0, wait)
+
+        @pl.loop(0, coarse_blocks - 1)
         def _(step):
-            compute(step)
-
-        @pl.when(jnp.logical_not(has_prev))
-        def _():
-            relay()
-
-        send(0, opening)
-
-        @pl.loop(coarse_blocks, blocks)
-        def _(step):
-            compute(step)
-
-        send(opening, middle)
-
-        @pl.when(has_prev)
-        def _():
-            relay()
-
-        send(middle, units)
-
-    @pl.when(jnp.logical_not(coarse_rank))
-    def _():
-        def after(unit):
-            @pl.when(unit == 0)
+            coarse_compute(step)
+
+    strips = columns // LANES // PARTS
+
+    @pl.loop(0, blocks + 1)
+    def _(step):
+        @pl.when(step == turn)
+        def _():
+            relay(0, coarse_blocks - 1)
+
+        @pl.when(coarse_rank & (step == jnp.minimum(turn, coarse_blocks - 1)))
+        def _():
+            coarse_compute(coarse_blocks - 1)
+
+        @pl.when(step == turn)
+        def _():
+            relay(coarse_blocks - 1, coarse_blocks)
+            send(PARTS * early, PARTS * turn)
+
+        @pl.when(step < blocks)
+        def _():
+            block = block_of(step)
+            in_coarse = coarse_rank & (step < coarse_blocks)
+
+            @pl.when(step >= jnp.where(coarse_rank, coarse_blocks, 1))
             def _():
-                greet()
-
-            send(unit, unit + 1)
-
-        @pl.loop(0, blocks)
-        def _(step):
-            compute(step, after)
-
-        @pl.when(jnp.logical_not(has_prev))
-        def _():
-            whole_start.wait()
+                load_step(step, wait)
+                halo_wait(block)
+
+            @pl.when(coarse_rank & (step == 0))
+            def _():
+                load_coarse(1, wait)
+                load_coarse(2, wait)
+
+            @pl.loop(0, PARTS)
+            def _(part):
+                @pl.when(jnp.logical_not(coarse_rank) & (step == 0))
+                def _():
+                    load_part(part, wait)
+
+                @pl.loop(0, strips)
+                def _(index):
+                    low = (part * strips + index) * LANES
+
+                    @pl.when(
+                        jnp.logical_not(in_coarse & (low >= low_column) & (low < low_column + CX))
+                    )
+                    def _():
+                        strip_compute(block, pl.multiple_of(low, LANES), False)
+
+                unit = PARTS * step + part
+
+                @pl.when(jnp.logical_not(coarse_rank) & (unit == 0))
+                def _():
+                    greet()
+
+                @pl.when((step < early) | (step >= turn))
+                def _():
+                    send(unit, unit + 1)
+
+    @pl.when(jnp.logical_not(has_prev))
+    def _():
+        begin_copies(wait)
 
     for side, exists in ((0, has_up), (1, has_down)):
 
@@ -457,8 +501,8 @@
             pltpu.VMEM((3, 2, slab + 2 * HALO, columns), jnp.float32),
             pltpu.VMEM((2, coarse_rows, CX), jnp.float32),
             pltpu.VMEM((2, coarse_rows, CX), jnp.float32),
-            dma((2, blocks)),
-            dma,
+            dma((2, PARTS + blocks)),
+            dma((3,)),
             dma((2, 2)),
             dma((2, 2)),
             dma((PARTS * blocks,)),

time: 54.2 us -> 54.1 us (level)
  no operation moved by 1% of the time
where the time goes in v1:
time: 54.1 us; the launch traced here: 54 us
  Pallas kernels  53.3 us (99%)
  between operations  0.64 us (1%)
    pallas_call x1, Pallas kernels, body(): pl.pallas_call(kernel, out_shape=(OUT((2, slab, columns), jnp.float32), O...  50.6 us
    pallas_call x1, Pallas kernels, body(): pl.pallas_call(write_out, out_shape=(jax.ShapeDtypeStruct(start.shape, jn...  2.72 us

profile of v1, /device:TPU:9, one launch (start us, length us, event | category | flops | bytes accessed | tf_op | source)
XLA Modules:
  0.0 54.0 jit_solution(10191287486024747801)
XLA Ops:
  0.6 50.6 %shard_map.41 = (f32[2,256,1024]{2,1,0:T(8,128)S(1)}, f32[2,2,256,1024]{3,2,1,0:T(8,128)S(1)}) custom-call(f32[2,256,1024]{2,1,0:T(8,128)} %bitcast.5, f32[2,2,256,1024]{3,2,1,0:T(8,128)} %bitcast.4), custom_call_target="tpu_custom_call" | custom-call | tf_op jit(solution)/shard_map/pallas_call | solution.py:492
  51.2 2.7 %shard_map.42 = (f32[2,256,1024]{2,1,0:T(8,128)}, f32[2,2,256,1024]{3,2,1,0:T(8,128)}) custom-call(f32[2,256,1024]{2,1,0:T(8,128)S(1)} %get-tuple-element.6.start, f32[2,2,256,1024]{3,2,1,0:T(8,128)S(1)} %get-tuple-element.7.nodes), custom_call_target="tpu_custom_call" | custom-call | tf_op jit(solution)/shard_map/pallas_call | solution.py:517

commit v2 on v1

--- a/solution.py
+++ b/solution.py
@@ -55,12 +55,12 @@
 ):
     slab, columns = begin_hbm.shape[1:]
     peers, count = lax.axis_size("space"), lax.axis_size("tm")
-    total = slab * peers
+    rows_total = slab * peers
     tm, rank = lax.axis_index("tm"), lax.axis_index("space")
     has_prev, has_next = tm > 0, tm < count - 1
     has_up, has_down = rank > 0, rank < peers - 1
     blocks = slab // BLOCK
-    low_row = total // 2 - CX // 2
+    low_row = rows_total // 2 - CX // 2
     low_column = columns // 2 - CX // 2
     coarse_rows = gain.shape[1]
     coarse_blocks = coarse_rows // BLOCK
@@ -74,7 +74,6 @@
         jnp.where(lower, coarse_block, blocks - coarse_block - coarse_blocks),
         0,
     )
-    ascending = lower != coarse_rank
 
     def block_of(step):
         index = jnp.where(step < blocks - first, first + step, blocks - 1 - step)
@@ -83,85 +82,87 @@
     def rows_of(block):
         return pl.ds(pl.multiple_of(block * BLOCK, BLOCK), BLOCK)
 
-    def load(slot, top, height, left, width, act):
+    def load(slot, top, height, left, width):
         top, left = pl.multiple_of(top, HALO), pl.multiple_of(left, LANES)
         source, here = pl.ds(top, height), pl.ds(left, width)
         target = pl.ds(pl.multiple_of(top + HALO, HALO), height)
-        act(
-            pltpu.make_async_copy(
-                begin_hbm.at[:, source, here], ext.at[0, :, target, here], load_sem.at[0, slot]
-            )
-        )
-        act(
-            pltpu.make_async_copy(
-                nodes_hbm.at[:, :, source, here],
-                ext.at[1:3, :, target, here],
-                load_sem.at[1, slot],
-            )
-        )
-
-    def load_step(step, act):
-        @pl.when(step < blocks - 1)
-        def _():
-            top = block_of(step) * BLOCK + jnp.where(ascending, HALO, -HALO)
-            load(PARTS + step, top, BLOCK, 0, columns, act)
-
-        @pl.when(step == blocks - 1)
-        def _():
-            height = BLOCK - HALO
-            load(PARTS + step, jnp.where(ascending, slab - height, 0), height, 0, columns, act)
-
-    def load_part(part, act):
-        height, width = BLOCK + HALO, columns // PARTS
-        load(part, jnp.where(ascending, 0, slab - height), height, part * width, width, act)
-
-    def load_coarse(slot, act):
-        height = coarse_rows + inward
-        top = jnp.where(lower, slab - height, 0)
-        if slot == 0:
-            load(0, top, height, low_column, CX, act)
-        else:
-            load(slot, top, height, (slot - 1) * (low_column + CX), low_column, act)
-
-    def begin_copies(act):
-        def copy(index, top, height, left, width):
+        pltpu.make_async_copy(
+            begin_hbm.at[:, source, here], ext.at[0, :, target, here], load_sem.at[slot]
+        ).start()
+        pltpu.make_async_copy(
+            nodes_hbm.at[:, :, source, here], ext.at[1:3, :, target, here], load_sem.at[slot]
+        ).start()
+
+    def loaded(slot, height, width):
+        part = ext.at[:, :, pl.ds(0, height), pl.ds(0, width)]
+        pltpu.make_async_copy(part, part, load_sem.at[slot]).wait()
+
+    side_rows = coarse_rows + inward
+    first_rows, width = BLOCK + HALO, columns // PARTS
+    rest_rows = slab - first_rows - BLOCK
+
+    def load_coarse_rank():
+        top = jnp.where(lower, slab - side_rows, 0)
+        load(0, top, side_rows, low_column, CX)
+        load(1, top, side_rows, 0, low_column)
+        load(1, top, side_rows, low_column + CX, low_column)
+        if slab > side_rows:
+            load(2, jnp.where(lower, 0, side_rows), slab - side_rows, 0, columns)
+
+    def load_other_rank():
+        @pl.loop(0, PARTS)
+        def _(part):
+            load(part, jnp.where(lower, 0, slab - first_rows), first_rows, part * width, width)
+
+        load(PARTS, jnp.where(lower, first_rows, rest_rows), BLOCK, 0, columns)
+        load(PARTS + 1, jnp.where(lower, slab - rest_rows, 0), rest_rows, 0, columns)
+
+    def begin_copies():
+        def copy(top, height, left, width):
             place = (slice(None), pl.ds(pl.multiple_of(top, HALO), height), pl.ds(left, width))
-            act(pltpu.make_async_copy(begin_hbm.at[place], start_out.at[place], start_sem.at[index]))
+            pltpu.make_async_copy(begin_hbm.at[place], start_out.at[place], start_sem).start()
 
         @pl.when(coarse_rank)
         def _():
-            copy(0, coarse_start, coarse_rows, 0, low_column)
-            copy(1, coarse_start, coarse_rows, low_column + CX, low_column)
+            copy(coarse_start, coarse_rows, 0, low_column)
+            copy(coarse_start, coarse_rows, low_column + CX, low_column)
             if slab > coarse_rows:
                 top = jnp.where(lower, 0, coarse_rows)
-                copy(2, top, slab - coarse_rows, 0, columns)
+                copy(top, slab - coarse_rows, 0, columns)
 
         @pl.when(jnp.logical_not(coarse_rank))
         def _():
-            copy(0, 0, slab, 0, columns)
-
-    def halos(side):
+            copy(0, slab, 0, columns)
+
+    def halo_start(side):
         source = pl.ds(0 if side == 0 else slab - HALO, HALO)
         target = pl.ds(slab + HALO if side == 0 else 0, HALO)
-        there = {"space": rank - 1 if side == 0 else rank + 1}
-        return (
-            pltpu.make_async_remote_copy(
-                begin_hbm.at[:, source, :],
-                ext.at[0, :, target, :],
-                halo_send.at[0, side],
-                halo_recv.at[0, side],
-                device_id=there,
-                device_id_type=MESH,
-            ),
-            pltpu.make_async_remote_copy(
-                nodes_hbm.at[:, :, source, :],
-                ext.at[1:3, :, target, :],
-                halo_send.at[1, side],
-                halo_recv.at[1, side],
-                device_id=there,
-                device_id_type=MESH,
-            ),
-        )
+        for slot, left, extent in (
+            (0, low_column, CX),
+            (1, 0, low_column),
+            (1, low_column + CX, low_column),
+        ):
+            here = pl.ds(left, extent)
+            for there_from, there_to in (
+                (begin_hbm.at[:, source, here], ext.at[0, :, target, here]),
+                (nodes_hbm.at[:, :, source, here], ext.at[1:3, :, target, here]),
+            ):
+                pltpu.make_async_remote_copy(
+                    there_from,
+                    there_to,
+                    halo_send.at[side],
+                    halo_recv.at[side, slot],
+                    device_id={"space": rank - 1 if side == 0 else rank + 1},
+                    device_id_type=MESH,
+                ).start()
+
+    def halo_wait(block, slot):
+        for side, edge in ((0, (block == blocks - 1) & has_down), (1, (block == 0) & has_up)):
+
+            @pl.when(edge)
+            def _(side=side):
+                part = ext.at[:, :, pl.ds(0, HALO), pl.ds(0, CX if slot == 0 else columns - CX)]
+                pltpu.make_async_copy(part, part, halo_recv.at[side, slot]).wait()
 
     following = {"tm": tm + 1}
 
@@ -170,29 +171,27 @@
         return pltpu.make_async_remote_copy(
             nodes_out.at[(1,) + place],
             start_out.at[place],
-            relay_send.at[step],
+            relay_send,
             relay_recv.at[step],
             device_id=following,
             device_id_type=MESH,
         )
 
-    def bulk(unit, act):
+    def bulk(unit):
         step, part = unit // PARTS, unit % PARTS
         block = block_of(step)
         strip = coarse_rank & (step < coarse_blocks)
 
         def copy(left, width):
             place = (slice(None), rows_of(block), pl.ds(pl.multiple_of(left, LANES), width))
-            act(
-                pltpu.make_async_remote_copy(
-                    nodes_out.at[(1,) + place],
-                    start_out.at[place],
-                    bulk_send.at[unit],
-                    bulk_recv.at[unit],
-                    device_id=following,
-                    device_id_type=MESH,
-                )
-            )
+            pltpu.make_async_remote_copy(
+                nodes_out.at[(1,) + place],
+                start_out.at[place],
+                bulk_send,
+                bulk_recv,
+                device_id=following,
+                device_id_type=MESH,
+            ).start()
 
         @pl.when(strip & (part >= PARTS - 2))
         def _():
@@ -213,7 +212,7 @@
         def _():
             @pl.loop(low, high)
             def _(unit):
-                bulk(unit, lambda c: c.start())
+                bulk(unit)
 
     barrier = pltpu.get_barrier_semaphore()
     for there, exists in (
@@ -227,26 +226,8 @@
         def _(there=there):
             pl.semaphore_signal(barrier, inc=1, device_id=there, device_id_type=MESH)
 
-    def start(copy):
-        copy.start()
-
-    def wait(copy):
-        copy.wait()
-
-    @pl.when(coarse_rank)
-    def _():
-        for slot in range(3):
-            load_coarse(slot, start)
-
-    @pl.when(jnp.logical_not(coarse_rank))
-    def _():
-        @pl.loop(0, PARTS)
-        def _(part):
-            load_part(part, start)
-
-    @pl.loop(jnp.where(coarse_rank, coarse_blocks, 1), blocks)
-    def _(step):
-        load_step(step, start)
+    pl.when(coarse_rank)(load_coarse_rank)
+    pl.when(jnp.logical_not(coarse_rank))(load_other_rank)
 
     for side, exists in ((0, has_up), (1, has_down)):
 
@@ -255,9 +236,7 @@
             edge = pl.ds(0 if side == 0 else slab + HALO, HALO)
             ext[:, :, edge, :] = jnp.zeros((3, 2, HALO, columns), jnp.float32)
 
-    @pl.when(jnp.logical_not(has_prev))
-    def _():
-        begin_copies(start)
+    pl.when(jnp.logical_not(has_prev))(begin_copies)
 
     def greet():
         friends = sum(jnp.where(e, 1, 0) for e in (has_up, has_down, has_prev, has_next))
@@ -266,16 +245,7 @@
 
             @pl.when(exists)
             def _(side=side):
-                for c in halos(side):
-                    c.start()
-
-    def halo_wait(block):
-        for side, edge in ((0, (block == blocks - 1) & has_down), (1, (block == 0) & has_up)):
-
-            @pl.when(edge)
-            def _(side=side):
-                for c in halos(side):
-                    c.wait_recv()
+                halo_start(side)
 
     def strip_compute(block, column, coarse):
         length = BLOCK + 2 * HALO
@@ -284,10 +254,10 @@
         begin, one, two = [[ext[f, k, span, here] for k in range(2)] for f in range(3)]
         row = lax.broadcasted_iota(jnp.int32, (length, LANES), 0)
         row = row + (rank * slab + block * BLOCK - HALO)
-        along = (row - total // 2).astype(jnp.float32) / (total // 2)
+        along = (row - rows_total // 2).astype(jnp.float32) / (rows_total // 2)
         place = lax.broadcasted_iota(jnp.int32, (1, LANES), 1) + column
         across = (place - columns // 2).astype(jnp.float32) / (columns // 2)
-        inside = jnp.where((row >= 0) & (row < total), 1.0, 0.0).astype(jnp.float32)
+        inside = jnp.where((row >= 0) & (row < rows_total), 1.0, 0.0).astype(jnp.float32)
         real = -diffusion * (along * along + across * across)
         imag = -drift * across
         factor = shear * across
@@ -336,7 +306,7 @@
 
     def coarse_compute(step):
         block = block_of(step)
-        halo_wait(block)
+        halo_wait(block, 0)
 
         @pl.loop(0, CX // LANES)
         def _(index):
@@ -366,7 +336,6 @@
             for k in range(2):
                 nodes_out[0, k, rows, here] += 0.5 * (begin[k] + finish[k])
 
-    units = PARTS * blocks
     never = blocks + 1
     turn = jnp.where(coarse_rank, jnp.minimum(TURN * tm, blocks), never)
     early = jnp.where(coarse_rank, jnp.minimum(tm // 2, turn), blocks)
@@ -374,7 +343,7 @@
     @pl.when(coarse_rank)
     def _():
         greet()
-        load_coarse(0, wait)
+        loaded(0, side_rows, CX)
 
         @pl.loop(0, coarse_blocks - 1)
         def _(step):
@@ -402,21 +371,33 @@
             block = block_of(step)
             in_coarse = coarse_rank & (step < coarse_blocks)
 
-            @pl.when(step >= jnp.where(coarse_rank, coarse_blocks, 1))
-            def _():
-                load_step(step, wait)
-                halo_wait(block)
-
             @pl.when(coarse_rank & (step == 0))
             def _():
-                load_coarse(1, wait)
-                load_coarse(2, wait)
+                loaded(1, side_rows, columns - CX)
+
+            if slab > side_rows:
+
+                @pl.when(coarse_rank & (step == coarse_blocks))
+                def _():
+                    loaded(2, slab - side_rows, columns)
+
+            for slot, height in ((PARTS, BLOCK), (PARTS + 1, rest_rows)):
+
+                @pl.when(jnp.logical_not(coarse_rank) & (step == slot - PARTS + 1))
+                def _(slot=slot, height=height):
+                    loaded(slot, height, columns)
+
+            @pl.when(jnp.logical_not(in_coarse))
+            def _():
+                halo_wait(block, 0)
+
+            halo_wait(block, 1)
 
             @pl.loop(0, PARTS)
             def _(part):
                 @pl.when(jnp.logical_not(coarse_rank) & (step == 0))
                 def _():
-                    load_part(part, wait)
+                    loaded(part, first_rows, width)
 
                 @pl.loop(0, strips)
                 def _(index):
@@ -438,54 +419,56 @@
                 def _():
                     send(unit, unit + 1)
 
+    def total(sem, height, extent):
+        part = start_out.at[:, pl.ds(0, height), pl.ds(0, extent)]
+        pltpu.make_async_copy(part, part, sem).wait()
+
+    def all_bulk(sem):
+        @pl.when(coarse_rank)
+        def _():
+            total(sem, slab - coarse_rows * CX // columns, columns)
+
+        @pl.when(jnp.logical_not(coarse_rank))
+        def _():
+            total(sem, slab, columns)
+
+    for side, exists in ((0, has_up), (1, has_down)):
+
+        @pl.when(exists)
+        def _(side=side):
+            part = ext.at[:, :, pl.ds(0, HALO), :]
+            pltpu.make_async_copy(part, part, halo_send.at[side]).wait()
+
+    @pl.when(coarse_rank & has_next)
+    def _():
+        total(relay_send, coarse_rows, CX)
+
     @pl.when(jnp.logical_not(has_prev))
     def _():
-        begin_copies(wait)
-
-    for side, exists in ((0, has_up), (1, has_down)):
-
-        @pl.when(exists)
-        def _(side=side):
-            for c in halos(side):
-                c.wait_send()
-
-    @pl.when(coarse_rank & has_next)
-    def _():
-        @pl.loop(0, coarse_blocks)
-        def _(step):
-            relay_copy(step).wait_send()
+        all_bulk(start_sem)
 
     @pl.when(has_prev)
     def _():
-        @pl.loop(0, units)
-        def _(unit):
-            bulk(unit, lambda c: c.wait_recv())
+        all_bulk(bulk_recv)
 
     @pl.when(has_next)
     def _():
-        @pl.loop(0, units)
-        def _(unit):
-            bulk(unit, lambda c: c.wait_send())
+        all_bulk(bulk_send)
 
 
 def write_out(start, nodes, start_hbm, nodes_hbm, sem):
-    copies = [
-        pltpu.make_async_copy(nodes.at[f, k], nodes_hbm.at[f, k], sem.at[2 * f + k])
-        for f in range(2)
-        for k in range(2)
-    ]
-    copies += [pltpu.make_async_copy(start.at[k], start_hbm.at[k], sem.at[4 + k]) for k in range(2)]
-    for c in copies:
-        c.start()
-    for c in copies:
-        c.wait()
+    for source, target, which in ((nodes, nodes_hbm, 0), (start, start_hbm, 1)):
+        for k in range(source.shape[0]):
+            pltpu.make_async_copy(source.at[k], target.at[k], sem.at[which]).start()
+    pltpu.make_async_copy(nodes, nodes_hbm, sem.at[0]).wait()
+    pltpu.make_async_copy(start, start_hbm, sem.at[1]).wait()
 
 
 def body(start_values, node_values):
     slab, columns = start_values.shape[2:]
     peers = lax.axis_size("space")
     coarse_rows = min(slab, max(CX // 2, CX // peers))
-    blocks, coarse_blocks = slab // BLOCK, coarse_rows // BLOCK
+    coarse_blocks = coarse_rows // BLOCK
     hbm = pl.BlockSpec(memory_space=pltpu.HBM)
     vmem = pl.BlockSpec(memory_space=pltpu.VMEM)
     dma = pltpu.SemaphoreType.DMA
@@ -501,13 +484,13 @@
             pltpu.VMEM((3, 2, slab + 2 * HALO, columns), jnp.float32),
             pltpu.VMEM((2, coarse_rows, CX), jnp.float32),
             pltpu.VMEM((2, coarse_rows, CX), jnp.float32),
-            dma((2, PARTS + blocks)),
-            dma((3,)),
+            dma((PARTS + 2,)),
+            dma,
+            dma((2,)),
             dma((2, 2)),
-            dma((2, 2)),
-            dma((PARTS * blocks,)),
-            dma((PARTS * blocks,)),
-            dma((coarse_blocks,)),
+            dma,
+            dma,
+            dma,
             dma((coarse_blocks,)),
         ],
         compiler_params=pltpu.CompilerParams(
@@ -522,7 +505,7 @@
         ),
         in_specs=[pl.BlockSpec(memory_space=pl.ANY)] * 2,
         out_specs=(hbm, hbm),
-        scratch_shapes=[dma((6,))],
+        scratch_shapes=[dma((2,))],
         compiler_params=pltpu.CompilerParams(vmem_limit_bytes=2 * 1024 * 1024),
     )(start, nodes)
     return (start[None], nodes[None])

time: 54.1 us -> 53.1 us (0.982)
  Pallas kernels: 53.3 us -> 52.3 us
    pallas_call x1, Pallas kernels: 50.6 us -> 49.6 us  [body(): pl.pallas_call(kernel, out_shape=(OUT((2, slab, columns), jnp.float32), O...]
where the time goes in v2:
time: 53.1 us; the launch traced here: 52.9 us
  Pallas kernels  52.3 us (98%)
  between operations  0.64 us (1%)
    pallas_call x1, Pallas kernels, body(): pl.pallas_call(kernel, out_shape=(OUT((2, slab, columns), jnp.float32), O...  49.6 us
    pallas_call x1, Pallas kernels, body(): pl.pallas_call(write_out, out_shape=(jax.ShapeDtypeStruct(start.shape, jn...  2.68 us

profile of v2, /device:TPU:9, one launch (start us, length us, event | category | flops | bytes accessed | tf_op | source)
XLA Modules:
  0.0 52.9 jit_solution(6936595817382870882)
XLA Ops:
  0.6 49.6 %shard_map.41 = (f32[2,256,1024]{2,1,0:T(8,128)S(1)}, f32[2,2,256,1024]{3,2,1,0:T(8,128)S(1)}) custom-call(f32[2,256,1024]{2,1,0:T(8,128)} %bitcast.5, f32[2,2,256,1024]{3,2,1,0:T(8,128)} %bitcast.4), custom_call_target="tpu_custom_call" | custom-call | tf_op jit(solution)/shard_map/pallas_call | solution.py:475
  50.2 2.7 %shard_map.42 = (f32[2,256,1024]{2,1,0:T(8,128)}, f32[2,2,256,1024]{3,2,1,0:T(8,128)}) custom-call(f32[2,256,1024]{2,1,0:T(8,128)S(1)} %get-tuple-element.6.start, f32[2,2,256,1024]{3,2,1,0:T(8,128)S(1)} %get-tuple-element.7.nodes), custom_call_target="tpu_custom_call" | custom-call | tf_op jit(solution)/shard_map/pallas_call | solution.py:500

commit v3 on v2

--- a/solution.py
+++ b/solution.py
@@ -1,3 +1,5 @@
+import functools
+
 import jax
 import jax.numpy as jnp
 from jax import lax
@@ -18,7 +20,10 @@
 HALO = 8
 BLOCK = 32
 PARTS = 4
-TURN = 3
+LATE = 4
+TURN = 2
+EARLY = 3
+PIECES = 4
 LANES = 128
 
 
@@ -34,6 +39,10 @@
     length = field[0].shape[0]
     sums = [pltpu.roll(f, 1, 0) + pltpu.roll(f, length - 1, 0) for f in field]
     return [factor * sums[1], -factor * sums[0]]
+
+
+def late(tm):
+    return tm >= LATE
 
 
 def kernel(
@@ -134,28 +143,42 @@
         def _():
             copy(0, slab, 0, columns)
 
-    def halo_start(side):
-        source = pl.ds(0 if side == 0 else slab - HALO, HALO)
+    def halo_start(side, slot, sources):
         target = pl.ds(slab + HALO if side == 0 else 0, HALO)
-        for slot, left, extent in (
-            (0, low_column, CX),
-            (1, 0, low_column),
-            (1, low_column + CX, low_column),
+        for left, extent in (
+            ((low_column, CX),)
+            if slot == 0
+            else ((0, low_column), (low_column + CX, low_column))
         ):
             here = pl.ds(left, extent)
-            for there_from, there_to in (
-                (begin_hbm.at[:, source, here], ext.at[0, :, target, here]),
-                (nodes_hbm.at[:, :, source, here], ext.at[1:3, :, target, here]),
-            ):
+            for source, place in zip(sources, (0, slice(1, 3))):
                 pltpu.make_async_remote_copy(
-                    there_from,
-                    there_to,
+                    source.at[..., here],
+                    ext.at[place, :, target, here],
                     halo_send.at[side],
                     halo_recv.at[side, slot],
                     device_id={"space": rank - 1 if side == 0 else rank + 1},
                     device_id_type=MESH,
                 ).start()
 
+    def halo_exchange(slots, loaded_edge):
+        for side, exists in ((0, has_up), (1, has_down)):
+            edge = pl.ds(0 if side == 0 else slab - HALO, HALO)
+            held = pl.ds(HALO if side == 0 else slab, HALO)
+            inner = coarse_rank & (lower if side == 1 else jnp.logical_not(lower))
+            for slot in slots:
+                fit = inner if loaded_edge else jnp.logical_not(inner)
+                fit = exists if slot == 1 else exists & fit
+                sources = (
+                    (ext.at[0, :, held, :], ext.at[1:3, :, held, :])
+                    if loaded_edge
+                    else (begin_hbm.at[:, edge, :], nodes_hbm.at[:, :, edge, :])
+                )
+
+                @pl.when(fit)
+                def _(side=side, slot=slot, sources=sources):
+                    halo_start(side, slot, sources)
+
     def halo_wait(block, slot):
         for side, edge in ((0, (block == blocks - 1) & has_down), (1, (block == 0) & has_up)):
 
@@ -166,8 +189,12 @@
 
     following = {"tm": tm + 1}
 
+    def relay_rows(step, origin):
+        top = block_of(step // PIECES) * BLOCK + step % PIECES * (BLOCK // PIECES) - origin
+        return pl.ds(pl.multiple_of(top, HALO), BLOCK // PIECES)
+
     def relay_copy(step):
-        place = (slice(None), rows_of(block_of(step)), pl.ds(low_column, CX))
+        place = (slice(None), relay_rows(step, 0), pl.ds(low_column, CX))
         return pltpu.make_async_remote_copy(
             nodes_out.at[(1,) + place],
             start_out.at[place],
@@ -203,16 +230,18 @@
         def _():
             copy(part * (columns // PARTS), columns // PARTS)
 
-        @pl.when(jnp.logical_not(quick | strip) & (part == PARTS - 1))
+        @pl.when(jnp.logical_not(quick | coarse_rank) & (part == PARTS - 1))
         def _():
             copy(0, columns)
 
-    def send(low, high):
-        @pl.when(has_next)
+    def send(step, low, high):
+        held = coarse_rank & late(tm) & (step == coarse_blocks - 1)
+
+        @pl.when(has_next & jnp.logical_not(held))
         def _():
             @pl.loop(low, high)
-            def _(unit):
-                bulk(unit)
+            def _(part):
+                bulk(PARTS * step + part)
 
     barrier = pltpu.get_barrier_semaphore()
     for there, exists in (
@@ -241,12 +270,6 @@
     def greet():
         friends = sum(jnp.where(e, 1, 0) for e in (has_up, has_down, has_prev, has_next))
         pl.semaphore_wait(barrier, friends)
-        for side, exists in ((0, has_up), (1, has_down)):
-
-            @pl.when(exists)
-            def _(side=side):
-                halo_start(side)
-
     def strip_compute(block, column, coarse):
         length = BLOCK + 2 * HALO
         span = pl.ds(pl.multiple_of(block * BLOCK, BLOCK), length)
@@ -319,9 +342,7 @@
             def _():
                 relay_copy(step).wait_recv()
 
-            block = block_of(step)
-            rows = rows_of(block)
-            local = pl.ds(pl.multiple_of(block * BLOCK - coarse_start, BLOCK), BLOCK)
+            rows, local = relay_rows(step, 0), relay_rows(step, coarse_start)
             here = pl.ds(low_column, CX)
             begin = [start_out[k, rows, here] for k in range(2)]
             grown = times(gain[0, local, :], gain[1, local, :], begin)
@@ -338,12 +359,14 @@
 
     never = blocks + 1
     turn = jnp.where(coarse_rank, jnp.minimum(TURN * tm, blocks), never)
-    early = jnp.where(coarse_rank, jnp.minimum(tm // 2, turn), blocks)
+    early = jnp.where(coarse_rank, jnp.minimum(EARLY * tm // 4, turn), blocks)
 
     @pl.when(coarse_rank)
     def _():
         greet()
         loaded(0, side_rows, CX)
+        halo_exchange((0,), True)
+        halo_exchange((0, 1), False)
 
         @pl.loop(0, coarse_blocks - 1)
         def _(step):
@@ -351,33 +374,41 @@
 
     strips = columns // LANES // PARTS
 
+    def step_at(index):
+        later = jnp.where(index == blocks - 1, coarse_blocks - 1, index + 1)
+        return jnp.where(coarse_rank & (index >= coarse_blocks - 1), later, index)
+
     @pl.loop(0, blocks + 1)
-    def _(step):
-        @pl.when(step == turn)
-        def _():
-            relay(0, coarse_blocks - 1)
-
-        @pl.when(coarse_rank & (step == jnp.minimum(turn, coarse_blocks - 1)))
+    def _(index):
+        @pl.when(index == turn)
+        def _():
+            relay(0, PIECES * (coarse_blocks - 1))
+
+        @pl.when(coarse_rank & (index == jnp.minimum(turn, coarse_blocks - 1)))
         def _():
             coarse_compute(coarse_blocks - 1)
 
-        @pl.when(step == turn)
-        def _():
-            relay(coarse_blocks - 1, coarse_blocks)
-            send(PARTS * early, PARTS * turn)
-
-        @pl.when(step < blocks)
-        def _():
+        @pl.when(index == turn)
+        def _():
+            relay(PIECES * (coarse_blocks - 1), PIECES * coarse_blocks)
+
+            @pl.loop(early, turn)
+            def _(position):
+                send(step_at(position), 0, PARTS)
+
+        @pl.when(index < blocks)
+        def _():
+            step = step_at(index)
             block = block_of(step)
             in_coarse = coarse_rank & (step < coarse_blocks)
 
-            @pl.when(coarse_rank & (step == 0))
+            @pl.when(coarse_rank & (index == 0))
             def _():
                 loaded(1, side_rows, columns - CX)
 
             if slab > side_rows:
 
-                @pl.when(coarse_rank & (step == coarse_blocks))
+                @pl.when(coarse_rank & (index == coarse_blocks - 1))
                 def _():
                     loaded(2, slab - side_rows, columns)
 
@@ -400,8 +431,8 @@
                     loaded(part, first_rows, width)
 
                 @pl.loop(0, strips)
-                def _(index):
-                    low = (part * strips + index) * LANES
+                def _(strip):
+                    low = (part * strips + strip) * LANES
 
                     @pl.when(
                         jnp.logical_not(in_coarse & (low >= low_column) & (low < low_column + CX))
@@ -409,24 +440,27 @@
                     def _():
                         strip_compute(block, pl.multiple_of(low, LANES), False)
 
-                unit = PARTS * step + part
-
-                @pl.when(jnp.logical_not(coarse_rank) & (unit == 0))
+                @pl.when(jnp.logical_not(coarse_rank) & (step == 0) & (part == 0))
                 def _():
                     greet()
-
-                @pl.when((step < early) | (step >= turn))
+                    halo_exchange((0, 1), False)
+
+                @pl.when((index < early) | (index >= turn))
                 def _():
-                    send(unit, unit + 1)
+                    send(step, part, part + 1)
 
     def total(sem, height, extent):
         part = start_out.at[:, pl.ds(0, height), pl.ds(0, extent)]
         pltpu.make_async_copy(part, part, sem).wait()
 
-    def all_bulk(sem):
-        @pl.when(coarse_rank)
-        def _():
-            total(sem, slab - coarse_rows * CX // columns, columns)
+    def all_bulk(sem, rows, lately):
+        for short in (False, True):
+
+            @pl.when(coarse_rank & (lately == short))
+            def _(short=short):
+                extent = rows - BLOCK if short else rows
+                narrow = coarse_rows - BLOCK if short else coarse_rows
+                total(sem, extent - narrow * CX // columns, columns)
 
         @pl.when(jnp.logical_not(coarse_rank))
         def _():
@@ -445,23 +479,137 @@
 
     @pl.when(jnp.logical_not(has_prev))
     def _():
-        all_bulk(start_sem)
+        all_bulk(start_sem, slab, tm < 0)
 
     @pl.when(has_prev)
     def _():
-        all_bulk(bulk_recv)
+        all_bulk(bulk_recv, coarse_rows, late(tm - 1))
 
     @pl.when(has_next)
     def _():
-        all_bulk(bulk_send)
-
-
-def write_out(start, nodes, start_hbm, nodes_hbm, sem):
-    for source, target, which in ((nodes, nodes_hbm, 0), (start, start_hbm, 1)):
-        for k in range(source.shape[0]):
-            pltpu.make_async_copy(source.at[k], target.at[k], sem.at[which]).start()
+        all_bulk(bulk_send, coarse_rows, late(tm))
+
+
+def place_of(slab, columns, coarse_rows):
+    peers, rank = lax.axis_size("space"), lax.axis_index("space")
+    low_row = slab * peers // 2 - CX // 2
+    coarse_rank = (rank * slab < low_row + CX) & (rank * slab + slab > low_row)
+    coarse_start = jnp.clip(low_row - rank * slab, 0, slab - coarse_rows)
+    lower = rank < peers // 2
+    other, edge = jnp.where(lower, 0, coarse_rows), jnp.where(lower, slab - BLOCK, 0)
+    return coarse_rank, coarse_start, pl.multiple_of(other, HALO), pl.multiple_of(edge, HALO)
+
+
+def sides(columns):
+    width = columns // 2 - CX // 2
+    return pl.ds(0, width), pl.ds(columns - width, width)
+
+
+def write_out(coarse_rows, start, nodes, start_hbm, nodes_hbm, _, sem):
+    slab, columns = start.shape[1:]
+    coarse_rank, coarse_start, _, _ = place_of(slab, columns, coarse_rows)
+    partly = coarse_rank & (lax.axis_index("tm") > 0)
+    for k in range(2):
+        pltpu.make_async_copy(nodes.at[k], nodes_hbm.at[k], sem.at[0]).start()
+
+    def copy(top, height, act):
+        here = (slice(None), pl.ds(pl.multiple_of(top, HALO), height), slice(None))
+        act(pltpu.make_async_copy(start.at[here], start_hbm.at[here], sem.at[1]))
+
+    for act in (lambda c: c.start(), lambda c: c.wait()):
+
+        @pl.when(partly)
+        def _(act=act):
+            copy(coarse_start, coarse_rows, act)
+
+        @pl.when(jnp.logical_not(partly))
+        def _(act=act):
+            copy(0, slab, act)
+
     pltpu.make_async_copy(nodes, nodes_hbm, sem.at[0]).wait()
-    pltpu.make_async_copy(start, start_hbm, sem.at[1]).wait()
+
+
+def send_rest(coarse_rows, nodes, _, rest_out, send_sem, recv_sem):
+    slab, columns = nodes.shape[2:]
+    coarse_rank, _, other, edge = place_of(slab, columns, coarse_rows)
+    tm, count = lax.axis_index("tm"), lax.axis_size("tm")
+    has_prev, has_next = coarse_rank & (tm > 0), coarse_rank & (tm < count - 1)
+    others = slab - coarse_rows
+    barrier = pltpu.get_barrier_semaphore()
+
+    def send(source, target):
+        pltpu.make_async_remote_copy(
+            source,
+            target,
+            send_sem,
+            recv_sem,
+            device_id={"tm": tm + 1},
+            device_id_type=MESH,
+        ).start()
+
+    def total(sem, lately):
+        for short in (False, True):
+
+            @pl.when(lately == short)
+            def _(short=short):
+                rows = others + (BLOCK - BLOCK * CX // columns if short else 0)
+                part = rest_out.at[:, pl.ds(0, rows), :]
+                pltpu.make_async_copy(part, part, sem).wait()
+
+    @pl.when(has_prev)
+    def _():
+        pl.semaphore_signal(barrier, inc=1, device_id={"tm": tm - 1}, device_id_type=MESH)
+
+    @pl.when(has_next)
+    def _():
+        pl.semaphore_wait(barrier, 1)
+
+        @pl.when(late(tm))
+        def _():
+            for side in sides(columns):
+                send(
+                    nodes.at[1, :, pl.ds(edge, BLOCK), side],
+                    rest_out.at[:, pl.ds(others, BLOCK), side],
+                )
+
+        send(nodes.at[1, :, pl.ds(other, others), :], rest_out.at[:, pl.ds(0, others), :])
+
+    @pl.when(has_prev)
+    def _():
+        total(recv_sem, late(tm - 1))
+
+    @pl.when(has_next)
+    def _():
+        total(send_sem, late(tm))
+
+
+def write_rest(coarse_rows, rest, _, start_hbm, sem):
+    slab, columns = start_hbm.shape[1:]
+    coarse_rank, _, other, edge = place_of(slab, columns, coarse_rows)
+    tm, others = lax.axis_index("tm"), slab - coarse_rows
+
+    @pl.when(coarse_rank & (tm > 0))
+    def _():
+        whole = pltpu.make_async_copy(
+            rest.at[:, pl.ds(0, others), :], start_hbm.at[:, pl.ds(other, others), :], sem.at[0]
+        )
+        strips = [
+            pltpu.make_async_copy(
+                rest.at[:, pl.ds(others, BLOCK), side],
+                start_hbm.at[:, pl.ds(edge, BLOCK), side],
+                sem.at[1 + index],
+            )
+            for index, side in enumerate(sides(columns))
+        ]
+        whole.start()
+        for act in (lambda c: c.start(), lambda c: c.wait()):
+
+            @pl.when(late(tm - 1))
+            def _(act=act):
+                for strip in strips:
+                    act(strip)
+
+        whole.wait()
 
 
 def body(start_values, node_values):
@@ -471,6 +619,7 @@
     coarse_blocks = coarse_rows // BLOCK
     hbm = pl.BlockSpec(memory_space=pltpu.HBM)
     vmem = pl.BlockSpec(memory_space=pltpu.VMEM)
+    anywhere = pl.BlockSpec(memory_space=pl.ANY)
     dma = pltpu.SemaphoreType.DMA
     start, nodes = pl.pallas_call(
         kernel,
@@ -491,24 +640,45 @@
             dma,
             dma,
             dma,
-            dma((coarse_blocks,)),
+            dma((PIECES * coarse_blocks,)),
         ],
         compiler_params=pltpu.CompilerParams(
             collective_id=0, has_side_effects=True, vmem_limit_bytes=56 * 1024 * 1024
         ),
     )(start_values[0], node_values[0])
-    start, nodes = pl.pallas_call(
-        write_out,
+    start_hbm, nodes_hbm, written = pl.pallas_call(
+        functools.partial(write_out, coarse_rows),
         out_shape=(
             jax.ShapeDtypeStruct(start.shape, jnp.float32),
             jax.ShapeDtypeStruct(nodes.shape, jnp.float32),
+            OUT((8, LANES), jnp.float32),
         ),
-        in_specs=[pl.BlockSpec(memory_space=pl.ANY)] * 2,
-        out_specs=(hbm, hbm),
+        in_specs=[anywhere, anywhere],
+        out_specs=(hbm, hbm, vmem),
         scratch_shapes=[dma((2,))],
         compiler_params=pltpu.CompilerParams(vmem_limit_bytes=2 * 1024 * 1024),
     )(start, nodes)
-    return (start[None], nodes[None])
+    if slab > coarse_rows:
+        rest = pl.pallas_call(
+            functools.partial(send_rest, coarse_rows),
+            out_shape=OUT((2, slab - coarse_rows + BLOCK, columns), jnp.float32),
+            in_specs=[anywhere, anywhere],
+            out_specs=vmem,
+            scratch_shapes=[dma, dma],
+            compiler_params=pltpu.CompilerParams(
+                collective_id=1, has_side_effects=True, vmem_limit_bytes=4 * 1024 * 1024
+            ),
+        )(nodes, written)
+        start_hbm = pl.pallas_call(
+            functools.partial(write_rest, coarse_rows),
+            out_shape=jax.ShapeDtypeStruct(start.shape, jnp.float32),
+            in_specs=[anywhere, hbm],
+            out_specs=hbm,
+            scratch_shapes=[dma((3,))],
+            input_output_aliases={1: 0},
+            compiler_params=pltpu.CompilerParams(vmem_limit_bytes=2 * 1024 * 1024),
+        )(rest, start_hbm)
+    return (start_hbm[None], nodes_hbm[None])
 
 
 OUT = pltpu.VMEM

time: 53.1 us -> 51.3 us (0.966)
  Pallas kernels: 52.3 us -> 50.4 us
    pallas_call x1, Pallas kernels: 49.6 us -> 29.6 us  [body(): pl.pallas_call(kernel, out_shape=(OUT((2, slab, columns), jnp.float32), O...]
    pallas_call x1 -> x3, Pallas kernels: 2.68 us -> 20.8 us  [the longest x1 17.4 us: body(): pl.pallas_call(functools.partial(send_rest, coarse_rows), out_shape=OUT((...]
where the time goes in v3:
time: 51.3 us; the launch traced here: 51.1 us
  Pallas kernels  50.4 us (98%)
  between operations  0.65 us (1%)
    pallas_call x1, Pallas kernels, body(): pl.pallas_call(kernel, out_shape=(OUT((2, slab, columns), jnp.float32), O...  29.6 us
    pallas_call x1, Pallas kernels, body(): pl.pallas_call(functools.partial(send_rest, coarse_rows), out_shape=OUT((...  17.4 us
    pallas_call x1, Pallas kernels, body(): pl.pallas_call(functools.partial(write_out, coarse_rows), out_shape=(jax....  2.37 us

profile of v3, /device:TPU:9, one launch (start us, length us, event | category | flops | bytes accessed | tf_op | source)
XLA Modules:
  0.0 51.1 jit_solution(4774071619849892537)
XLA Ops:
  0.6 29.6 %shard_map.41 = (f32[2,256,1024]{2,1,0:T(8,128)S(1)}, f32[2,2,256,1024]{3,2,1,0:T(8,128)S(1)}) custom-call(f32[2,256,1024]{2,1,0:T(8,128)} %bitcast.5, f32[2,2,256,1024]{3,2,1,0:T(8,128)} %bitcast.4), custom_call_target="tpu_custom_call" | custom-call | tf_op jit(solution)/shard_map/pallas_call | solution.py:624
  30.3 2.4 %shard_map.42 = (f32[2,256,1024]{2,1,0:T(8,128)}, f32[2,2,256,1024]{3,2,1,0:T(8,128)}, f32[8,128]{1,0:T(8,128)S(1)}) custom-call(f32[2,256,1024]{2,1,0:T(8,128)S(1)} %get-tuple-element.8.start, f32[2,2,256,1024]{3,2,1,0:T(8,128)S(1)} %get-tuple-element.7.nodes), custom_call_target="tpu_custom_call" | custom-call | tf_op jit(solution)/shard_map/pallas_call | solution.py:649
  32.7 17.4 %shard_map.43.rest = f32[2,160,1024]{2,1,0:T(8,128)S(1)} custom-call(f32[2,2,256,1024]{3,2,1,0:T(8,128)S(1)} %get-tuple-element.7.nodes, f32[8,128]{1,0:T(8,128)S(1)} %get-tuple-element.9._), custom_call_target="tpu_custom_call" | custom-call | tf_op jit(solution)/shard_map/pallas_call | solution.py:662
  50.1 1.0 %shard_map.44 = f32[2,256,1024]{2,1,0:T(8,128)} custom-call(f32[2,160,1024]{2,1,0:T(8,128)S(1)} %shard_map.43.rest, f32[2,256,1024]{2,1,0:T(8,128)} %get-tuple-element.10._), custom_call_target="tpu_custom_call", output_to_operand_aliasing={{}: (1, {})} | custom-call | tf_op jit(solution)/shard_map/pallas_call | solution.py:672

commit v4 on v3

--- a/solution.py
+++ b/solution.py
@@ -21,6 +21,8 @@
 BLOCK = 32
 PARTS = 4
 LATE = 4
+DETOURS = 3
+DETOUR_ROWS = 16
 TURN = 2
 EARLY = 3
 PIECES = 4
@@ -61,6 +63,11 @@
     bulk_recv,
     relay_send,
     relay_recv,
+    transit,
+    transit_recv,
+    forward_send,
+    below,
+    above,
 ):
     slab, columns = begin_hbm.shape[1:]
     peers, count = lax.axis_size("space"), lax.axis_size("tm")
@@ -107,13 +114,17 @@
         pltpu.make_async_copy(part, part, load_sem.at[slot]).wait()
 
     side_rows = coarse_rows + inward
+    head_rows = BLOCK + 2 * HALO if inward else 0
     first_rows, width = BLOCK + HALO, columns // PARTS
     rest_rows = slab - first_rows - BLOCK
 
     def load_coarse_rank():
         top = jnp.where(lower, slab - side_rows, 0)
+        if head_rows:
+            load(3, jnp.where(lower, top, side_rows - head_rows), head_rows, 0, low_column)
         load(0, top, side_rows, low_column, CX)
-        load(1, top, side_rows, 0, low_column)
+        rest = jnp.where(lower, top + head_rows, 0)
+        load(1, rest, side_rows - head_rows, 0, low_column)
         load(1, top, side_rows, low_column + CX, low_column)
         if slab > side_rows:
             load(2, jnp.where(lower, 0, side_rows), slab - side_rows, 0, columns)
@@ -204,23 +215,78 @@
             device_id_type=MESH,
         )
 
+    detours = min(DETOURS, (count - 1) // 2)
+    taking_part = jnp.logical_not(coarse_rank) & (tm <= 2 * detours)
+    detoured = taking_part & (tm % 2 == 1)
+    detour_rows = transit.shape[2]
+
+    def detour_place():
+        top = pl.multiple_of(block_of(blocks - 1) * BLOCK, BLOCK)
+        return slice(None), pl.ds(top, detour_rows), slice(None)
+
+    def detour():
+        for sign, met, ends in ((1, below, (tm == 0, tm == 2 * detours)), (-1, above, (tm == 2 * detours, tm == 0))):
+
+            @pl.when(jnp.logical_not(ends[0]))
+            def _(met=met):
+                pl.semaphore_wait(met, 1)
+
+            @pl.when(jnp.logical_not(ends[1]))
+            def _(met=met, sign=sign):
+                pl.semaphore_signal(
+                    met, inc=1, device_id={"tm": tm + sign}, device_id_type=MESH
+                )
+
+        slot = tm // 2
+        place = detour_place()
+
+        @pl.when(detoured)
+        def _():
+            pltpu.make_async_remote_copy(
+                nodes_out.at[(1,) + place],
+                transit.at[slot],
+                bulk_send,
+                transit_recv.at[slot],
+                device_id={"tm": tm - tm},
+                device_id_type=MESH,
+            ).start()
+
+        @pl.when(tm == 0)
+        def _():
+            for slot in range(detours):
+                pltpu.make_async_copy(transit.at[slot], transit.at[slot], transit_recv.at[slot]).wait()
+                pltpu.make_async_remote_copy(
+                    transit.at[slot],
+                    start_out.at[place],
+                    forward_send,
+                    bulk_recv,
+                    device_id={"tm": tm + 2 * slot + 2},
+                    device_id_type=MESH,
+                ).start()
+            pltpu.make_async_copy(transit, transit, forward_send).wait()
+
+    def bulk_copy(block, left, width, top=0):
+        rows = pl.ds(pl.multiple_of(block * BLOCK + top, HALO), BLOCK - top)
+        place = (slice(None), rows, pl.ds(pl.multiple_of(left, LANES), width))
+        pltpu.make_async_remote_copy(
+            nodes_out.at[(1,) + place],
+            start_out.at[place],
+            bulk_send,
+            bulk_recv,
+            device_id=following,
+            device_id_type=MESH,
+        ).start()
+
     def bulk(unit):
         step, part = unit // PARTS, unit % PARTS
         block = block_of(step)
         strip = coarse_rank & (step < coarse_blocks)
+        sent = (step == 0) & (part == PARTS - 2) & (head_rows > 0)
 
         def copy(left, width):
-            place = (slice(None), rows_of(block), pl.ds(pl.multiple_of(left, LANES), width))
-            pltpu.make_async_remote_copy(
-                nodes_out.at[(1,) + place],
-                start_out.at[place],
-                bulk_send,
-                bulk_recv,
-                device_id=following,
-                device_id_type=MESH,
-            ).start()
-
-        @pl.when(strip & (part >= PARTS - 2))
+            bulk_copy(block, left, width)
+
+        @pl.when(strip & (part >= PARTS - 2) & jnp.logical_not(sent))
         def _():
             copy((part - (PARTS - 2)) * (low_column + CX), low_column)
 
@@ -230,9 +296,16 @@
         def _():
             copy(part * (columns // PARTS), columns // PARTS)
 
-        @pl.when(jnp.logical_not(quick | coarse_rank) & (part == PARTS - 1))
+        whole = jnp.logical_not(quick | coarse_rank) & (part == PARTS - 1)
+        short = detoured & (step == blocks - 1)
+
+        @pl.when(whole & jnp.logical_not(short))
         def _():
             copy(0, columns)
+
+        @pl.when(whole & short)
+        def _():
+            bulk_copy(block, 0, columns, detour_rows)
 
     def send(step, low, high):
         held = coarse_rank & late(tm) & (step == coarse_blocks - 1)
@@ -363,7 +436,20 @@
 
     @pl.when(coarse_rank)
     def _():
-        greet()
+        if head_rows:
+            loaded(3, head_rows, low_column)
+
+            @pl.loop(0, low_column // LANES)
+            def _(strip):
+                left = pl.multiple_of(strip * LANES, LANES)
+                strip_compute(block_of(0), left, False)
+                pl.when(strip == 0)(greet)
+
+                @pl.when(has_next)
+                def _():
+                    bulk_copy(block_of(0), left, LANES)
+        else:
+            greet()
         loaded(0, side_rows, CX)
         halo_exchange((0,), True)
         halo_exchange((0, 1), False)
@@ -404,7 +490,10 @@
 
             @pl.when(coarse_rank & (index == 0))
             def _():
-                loaded(1, side_rows, columns - CX)
+                if head_rows:
+                    loaded(1, 2 * side_rows - head_rows, low_column)
+                else:
+                    loaded(1, side_rows, columns - CX)
 
             if slab > side_rows:
 
@@ -434,9 +523,10 @@
                 def _(strip):
                     low = (part * strips + strip) * LANES
 
-                    @pl.when(
-                        jnp.logical_not(in_coarse & (low >= low_column) & (low < low_column + CX))
-                    )
+                    begun = in_coarse & (step == 0) & (low < low_column) & (head_rows > 0)
+                    kept = in_coarse & (low >= low_column) & (low < low_column + CX)
+
+                    @pl.when(jnp.logical_not(begun | kept))
                     def _():
                         strip_compute(block, pl.multiple_of(low, LANES), False)
 
@@ -448,6 +538,9 @@
                 @pl.when((index < early) | (index >= turn))
                 def _():
                     send(step, part, part + 1)
+
+    if detours:
+        pl.when(taking_part)(detour)
 
     def total(sem, height, extent):
         part = start_out.at[:, pl.ds(0, height), pl.ds(0, extent)]
@@ -617,6 +710,7 @@
     peers = lax.axis_size("space")
     coarse_rows = min(slab, max(CX // 2, CX // peers))
     coarse_blocks = coarse_rows // BLOCK
+    slots = max(1, min(DETOURS, (lax.axis_size("tm") - 1) // 2))
     hbm = pl.BlockSpec(memory_space=pltpu.HBM)
     vmem = pl.BlockSpec(memory_space=pltpu.VMEM)
     anywhere = pl.BlockSpec(memory_space=pl.ANY)
@@ -641,6 +735,11 @@
             dma,
             dma,
             dma((PIECES * coarse_blocks,)),
+            pltpu.VMEM((slots, 2, DETOUR_ROWS, columns), jnp.float32),
+            dma((slots,)),
+            dma,
+            pltpu.SemaphoreType.REGULAR,
+            pltpu.SemaphoreType.REGULAR,
         ],
         compiler_params=pltpu.CompilerParams(
             collective_id=0, has_side_effects=True, vmem_limit_bytes=56 * 1024 * 1024

time: 51.3 us -> 50 us (0.975); the launches traced: 51.1 us -> 49.1 us
  Pallas kernels: 50.4 us -> 48.4 us
    pallas_call x1, Pallas kernels: 29.6 us -> 28.2 us  [body(): pl.pallas_call(kernel, out_shape=(OUT((2, slab, columns), jnp.float32), O...]
    pallas_call x1, Pallas kernels: 17.4 us -> 16.9 us  [body(): pl.pallas_call(functools.partial(send_rest, coarse_rows), out_shape=OUT((...]
where the time goes in v4:
time: 50 us; the launch traced here: 49.1 us
  Pallas kernels  48.4 us (97%)
  between operations  0.65 us (1%)
    pallas_call x1, Pallas kernels, body(): pl.pallas_call(kernel, out_shape=(OUT((2, slab, columns), jnp.float32), O...  28.2 us
    pallas_call x1, Pallas kernels, body(): pl.pallas_call(functools.partial(send_rest, coarse_rows), out_shape=OUT((...  16.9 us
    pallas_call x1, Pallas kernels, body(): pl.pallas_call(functools.partial(write_out, coarse_rows), out_shape=(jax....  2.37 us
    pallas_call x1, Pallas kernels, body(): pl.pallas_call(functools.partial(write_rest, coarse_rows), out_shape=jax....  1.01 us

profile of v4, /device:TPU:9, one launch (start us, length us, event | category | flops | bytes accessed | tf_op | source)
XLA Modules:
  0.0 49.1 jit_solution(3824512186532259049)
XLA Ops:
  0.6 28.2 %shard_map.41 = (f32[2,256,1024]{2,1,0:T(8,128)S(1)}, f32[2,2,256,1024]{3,2,1,0:T(8,128)S(1)}) custom-call(f32[2,256,1024]{2,1,0:T(8,128)} %bitcast.5, f32[2,2,256,1024]{3,2,1,0:T(8,128)} %bitcast.4), custom_call_target="tpu_custom_call" | custom-call | tf_op jit(solution)/shard_map/pallas_call | solution.py:718
  28.8 2.4 %shard_map.42 = (f32[2,256,1024]{2,1,0:T(8,128)}, f32[2,2,256,1024]{3,2,1,0:T(8,128)}, f32[8,128]{1,0:T(8,128)S(1)}) custom-call(f32[2,256,1024]{2,1,0:T(8,128)S(1)} %get-tuple-element.8.start, f32[2,2,256,1024]{3,2,1,0:T(8,128)S(1)} %get-tuple-element.7.nodes), custom_call_target="tpu_custom_call" | custom-call | tf_op jit(solution)/shard_map/pallas_call | solution.py:748
  31.2 16.9 %shard_map.43.rest = f32[2,160,1024]{2,1,0:T(8,128)S(1)} custom-call(f32[2,2,256,1024]{3,2,1,0:T(8,128)S(1)} %get-tuple-element.7.nodes, f32[8,128]{1,0:T(8,128)S(1)} %get-tuple-element.9._), custom_call_target="tpu_custom_call" | custom-call | tf_op jit(solution)/shard_map/pallas_call | solution.py:761
  48.1 1.0 %shard_map.44 = f32[2,256,1024]{2,1,0:T(8,128)} custom-call(f32[2,160,1024]{2,1,0:T(8,128)S(1)} %shard_map.43.rest, f32[2,256,1024]{2,1,0:T(8,128)} %get-tuple-element.10._), custom_call_target="tpu_custom_call", output_to_operand_aliasing={{}: (1, {})} | custom-call | tf_op jit(solution)/shard_map/pallas_call | solution.py:771

commit v5 on v4

--- a/solution.py
+++ b/solution.py
@@ -20,7 +20,8 @@
 HALO = 8
 BLOCK = 32
 PARTS = 4
-LATE = 4
+DEFER = 5
+WRITES = 2
 DETOURS = 3
 DETOUR_ROWS = 16
 TURN = 2
@@ -43,8 +44,8 @@
     return [factor * sums[1], -factor * sums[0]]
 
 
-def late(tm):
-    return tm >= LATE
+def defers(tm, slab, coarse_rows):
+    return tm < DEFER if slab > coarse_rows else tm < 0
 
 
 def kernel(
@@ -56,7 +57,6 @@
     gain,
     shift,
     load_sem,
-    start_sem,
     halo_send,
     halo_recv,
     bulk_send,
@@ -65,9 +65,9 @@
     relay_recv,
     transit,
     transit_recv,
-    forward_send,
     below,
     above,
+    answer,
 ):
     slab, columns = begin_hbm.shape[1:]
     peers, count = lax.axis_size("space"), lax.axis_size("tm")
@@ -118,21 +118,30 @@
     first_rows, width = BLOCK + HALO, columns // PARTS
     rest_rows = slab - first_rows - BLOCK
 
+    def load_first():
+        top = jnp.where(lower, slab - side_rows, 0)
+        if head_rows:
+            load(3, jnp.where(lower, top, side_rows - head_rows), head_rows, 0, LANES)
+        else:
+            load(0, top, side_rows, low_column, CX)
+
     def load_coarse_rank():
         top = jnp.where(lower, slab - side_rows, 0)
         if head_rows:
-            load(3, jnp.where(lower, top, side_rows - head_rows), head_rows, 0, low_column)
-        load(0, top, side_rows, low_column, CX)
+            first_top = jnp.where(lower, top, side_rows - head_rows)
+            load(4, first_top, head_rows, LANES, low_column - LANES)
+            load(0, top, side_rows, low_column, CX)
         rest = jnp.where(lower, top + head_rows, 0)
         load(1, rest, side_rows - head_rows, 0, low_column)
         load(1, top, side_rows, low_column + CX, low_column)
         if slab > side_rows:
             load(2, jnp.where(lower, 0, side_rows), slab - side_rows, 0, columns)
 
+    def load_part(part):
+        load(part, jnp.where(lower, 0, slab - first_rows), first_rows, part * width, width)
+
     def load_other_rank():
-        @pl.loop(0, PARTS)
-        def _(part):
-            load(part, jnp.where(lower, 0, slab - first_rows), first_rows, part * width, width)
+        pl.loop(1, PARTS)(load_part)
 
         load(PARTS, jnp.where(lower, first_rows, rest_rows), BLOCK, 0, columns)
         load(PARTS + 1, jnp.where(lower, slab - rest_rows, 0), rest_rows, 0, columns)
@@ -140,7 +149,7 @@
     def begin_copies():
         def copy(top, height, left, width):
             place = (slice(None), pl.ds(pl.multiple_of(top, HALO), height), pl.ds(left, width))
-            pltpu.make_async_copy(begin_hbm.at[place], start_out.at[place], start_sem).start()
+            pltpu.make_async_copy(begin_hbm.at[place], start_out.at[place], bulk_recv).start()
 
         @pl.when(coarse_rank)
         def _():
@@ -172,6 +181,11 @@
                     device_id_type=MESH,
                 ).start()
 
+    def answered():
+        @pl.when(has_down)
+        def _():
+            pl.semaphore_wait(answer, 1)
+
     def halo_exchange(slots, loaded_edge):
         for side, exists in ((0, has_up), (1, has_down)):
             edge = pl.ds(0 if side == 0 else slab - HALO, HALO)
@@ -200,6 +214,9 @@
 
     following = {"tm": tm + 1}
 
+    def deferred(tm):
+        return defers(tm, slab, coarse_rows)
+
     def relay_rows(step, origin):
         top = block_of(step // PIECES) * BLOCK + step % PIECES * (BLOCK // PIECES) - origin
         return pl.ds(pl.multiple_of(top, HALO), BLOCK // PIECES)
@@ -246,24 +263,24 @@
                 nodes_out.at[(1,) + place],
                 transit.at[slot],
                 bulk_send,
-                transit_recv.at[slot],
+                transit_recv,
                 device_id={"tm": tm - tm},
                 device_id_type=MESH,
             ).start()
 
         @pl.when(tm == 0)
         def _():
+            pltpu.make_async_copy(transit, transit, transit_recv).wait()
             for slot in range(detours):
-                pltpu.make_async_copy(transit.at[slot], transit.at[slot], transit_recv.at[slot]).wait()
                 pltpu.make_async_remote_copy(
                     transit.at[slot],
                     start_out.at[place],
-                    forward_send,
+                    relay_send,
                     bulk_recv,
                     device_id={"tm": tm + 2 * slot + 2},
                     device_id_type=MESH,
                 ).start()
-            pltpu.make_async_copy(transit, transit, forward_send).wait()
+            pltpu.make_async_copy(transit, transit, relay_send).wait()
 
     def bulk_copy(block, left, width, top=0):
         rows = pl.ds(pl.multiple_of(block * BLOCK + top, HALO), BLOCK - top)
@@ -308,7 +325,7 @@
             bulk_copy(block, 0, columns, detour_rows)
 
     def send(step, low, high):
-        held = coarse_rank & late(tm) & (step == coarse_blocks - 1)
+        held = coarse_rank & deferred(tm) & (step == coarse_blocks - 1)
 
         @pl.when(has_next & jnp.logical_not(held))
         def _():
@@ -316,12 +333,16 @@
             def _(part):
                 bulk(PARTS * step + part)
 
+    pl.when(coarse_rank)(load_first)
+
+    @pl.when(jnp.logical_not(coarse_rank))
+    def _():
+        load_part(0)
+
     barrier = pltpu.get_barrier_semaphore()
     for there, exists in (
-        ({"space": rank - 1}, has_up),
+        ({"tm": tm - 1}, has_prev),
         ({"space": rank + 1}, has_down),
-        ({"tm": tm - 1}, has_prev),
-        ({"tm": tm + 1}, has_next),
     ):
 
         @pl.when(exists)
@@ -341,8 +362,17 @@
     pl.when(jnp.logical_not(has_prev))(begin_copies)
 
     def greet():
-        friends = sum(jnp.where(e, 1, 0) for e in (has_up, has_down, has_prev, has_next))
-        pl.semaphore_wait(barrier, friends)
+        friends = jnp.where(has_up, 1, 0) + jnp.where(has_next, 1, 0)
+
+        @pl.when(friends > 0)
+        def _():
+            pl.semaphore_wait(barrier, friends)
+
+        @pl.when(has_up)
+        def _():
+            pl.semaphore_signal(
+                answer, inc=1, device_id={"space": rank - 1}, device_id_type=MESH
+            )
     def strip_compute(block, column, coarse):
         length = BLOCK + 2 * HALO
         span = pl.ds(pl.multiple_of(block * BLOCK, BLOCK), length)
@@ -432,12 +462,12 @@
 
     never = blocks + 1
     turn = jnp.where(coarse_rank, jnp.minimum(TURN * tm, blocks), never)
-    early = jnp.where(coarse_rank, jnp.minimum(EARLY * tm // 4, turn), blocks)
+    early = jnp.where(coarse_rank, jnp.where(deferred(tm), jnp.minimum(EARLY * tm // 4, turn), turn), blocks)
 
     @pl.when(coarse_rank)
     def _():
         if head_rows:
-            loaded(3, head_rows, low_column)
+            loaded(3, head_rows, LANES)
 
             @pl.loop(0, low_column // LANES)
             def _(strip):
@@ -448,9 +478,14 @@
                 @pl.when(has_next)
                 def _():
                     bulk_copy(block_of(0), left, LANES)
+
+                @pl.when(strip == 0)
+                def _():
+                    loaded(4, head_rows, low_column - LANES)
         else:
             greet()
         loaded(0, side_rows, CX)
+        answered()
         halo_exchange((0,), True)
         halo_exchange((0, 1), False)
 
@@ -533,6 +568,10 @@
                 @pl.when(jnp.logical_not(coarse_rank) & (step == 0) & (part == 0))
                 def _():
                     greet()
+
+                @pl.when(jnp.logical_not(coarse_rank) & (step == 0) & (part == 1))
+                def _():
+                    answered()
                     halo_exchange((0, 1), False)
 
                 @pl.when((index < early) | (index >= turn))
@@ -572,15 +611,15 @@
 
     @pl.when(jnp.logical_not(has_prev))
     def _():
-        all_bulk(start_sem, slab, tm < 0)
+        all_bulk(bulk_recv, slab, tm < 0)
 
     @pl.when(has_prev)
     def _():
-        all_bulk(bulk_recv, coarse_rows, late(tm - 1))
+        all_bulk(bulk_recv, coarse_rows, deferred(tm - 1))
 
     @pl.when(has_next)
     def _():
-        all_bulk(bulk_send, coarse_rows, late(tm))
+        all_bulk(bulk_send, coarse_rows, deferred(tm))
 
 
 def place_of(slab, columns, coarse_rows):
@@ -602,8 +641,10 @@
     slab, columns = start.shape[1:]
     coarse_rank, coarse_start, _, _ = place_of(slab, columns, coarse_rows)
     partly = coarse_rank & (lax.axis_index("tm") > 0)
-    for k in range(2):
-        pltpu.make_async_copy(nodes.at[k], nodes_hbm.at[k], sem.at[0]).start()
+    for part in range(4 * WRITES):
+        height = slab // WRITES
+        here = (part // 2 % 2, part % 2, pl.ds(part // 4 * height, height))
+        pltpu.make_async_copy(nodes.at[here], nodes_hbm.at[here], sem.at[0]).start()
 
     def copy(top, height, act):
         here = (slice(None), pl.ds(pl.multiple_of(top, HALO), height), slice(None))
@@ -657,7 +698,7 @@
     def _():
         pl.semaphore_wait(barrier, 1)
 
-        @pl.when(late(tm))
+        @pl.when(defers(tm, slab, coarse_rows))
         def _():
             for side in sides(columns):
                 send(
@@ -669,11 +710,11 @@
 
     @pl.when(has_prev)
     def _():
-        total(recv_sem, late(tm - 1))
+        total(recv_sem, defers(tm - 1, slab, coarse_rows))
 
     @pl.when(has_next)
     def _():
-        total(send_sem, late(tm))
+        total(send_sem, defers(tm, slab, coarse_rows))
 
 
 def write_rest(coarse_rows, rest, _, start_hbm, sem):
@@ -694,10 +735,17 @@
             )
             for index, side in enumerate(sides(columns))
         ]
-        whole.start()
+        for part in range(2 * WRITES):
+            height = others // WRITES
+            top = part // 2 * height
+            pltpu.make_async_copy(
+                rest.at[part % 2, pl.ds(top, height), :],
+                start_hbm.at[part % 2, pl.ds(pl.multiple_of(other + top, HALO), height), :],
+                sem.at[0],
+            ).start()
         for act in (lambda c: c.start(), lambda c: c.wait()):
 
-            @pl.when(late(tm - 1))
+            @pl.when(defers(tm - 1, slab, coarse_rows))
             def _(act=act):
                 for strip in strips:
                     act(strip)
@@ -728,7 +776,6 @@
             pltpu.VMEM((2, coarse_rows, CX), jnp.float32),
             pltpu.VMEM((2, coarse_rows, CX), jnp.float32),
             dma((PARTS + 2,)),
-            dma,
             dma((2,)),
             dma((2, 2)),
             dma,
@@ -736,8 +783,8 @@
             dma,
             dma((PIECES * coarse_blocks,)),
             pltpu.VMEM((slots, 2, DETOUR_ROWS, columns), jnp.float32),
-            dma((slots,)),
             dma,
+            pltpu.SemaphoreType.REGULAR,
             pltpu.SemaphoreType.REGULAR,
             pltpu.SemaphoreType.REGULAR,
         ],

time: 50 us -> 49.4 us (0.988)
    pallas_call x1, Pallas kernels: 28.2 us -> 24.9 us  [body(): pl.pallas_call(kernel, out_shape=(OUT((2, slab, columns), jnp.float32), O...]
    pallas_call x1, Pallas kernels: 16.9 us -> 19.7 us  [body(): pl.pallas_call(functools.partial(send_rest, coarse_rows), out_shape=OUT((...]
where the time goes in v5:
time: 49.4 us; the launch traced here: 48.7 us
  Pallas kernels  48.1 us (97%)
  between operations  0.65 us (1%)
    pallas_call x1, Pallas kernels, body(): pl.pallas_call(kernel, out_shape=(OUT((2, slab, columns), jnp.float32), O...  24.9 us
    pallas_call x1, Pallas kernels, body(): pl.pallas_call(functools.partial(send_rest, coarse_rows), out_shape=OUT((...  19.7 us
    pallas_call x1, Pallas kernels, body(): pl.pallas_call(functools.partial(write_out, coarse_rows), out_shape=(jax....  2.37 us
    pallas_call x1, Pallas kernels, body(): pl.pallas_call(functools.partial(write_rest, coarse_rows), out_shape=jax....  1.06 us

profile of v5, /device:TPU:9, one launch (start us, length us, event | category | flops | bytes accessed | tf_op | source)
XLA Modules:
  0.0 48.7 jit_solution(9704189481921137216)
XLA Ops:
  0.6 24.9 %shard_map.41 = (f32[2,256,1024]{2,1,0:T(8,128)S(1)}, f32[2,2,256,1024]{3,2,1,0:T(8,128)S(1)}) custom-call(f32[2,256,1024]{2,1,0:T(8,128)} %bitcast.5, f32[2,2,256,1024]{3,2,1,0:T(8,128)} %bitcast.4), custom_call_target="tpu_custom_call" | custom-call | tf_op jit(solution)/shard_map/pallas_call | solution.py:766
  25.5 2.4 %shard_map.42 = (f32[2,256,1024]{2,1,0:T(8,128)}, f32[2,2,256,1024]{3,2,1,0:T(8,128)}, f32[8,128]{1,0:T(8,128)S(1)}) custom-call(f32[2,256,1024]{2,1,0:T(8,128)S(1)} %get-tuple-element.8.start, f32[2,2,256,1024]{3,2,1,0:T(8,128)S(1)} %get-tuple-element.7.nodes), custom_call_target="tpu_custom_call" | custom-call | tf_op jit(solution)/shard_map/pallas_call | solution.py:795
  27.9 19.7 %shard_map.43.rest = f32[2,160,1024]{2,1,0:T(8,128)S(1)} custom-call(f32[2,2,256,1024]{3,2,1,0:T(8,128)S(1)} %get-tuple-element.7.nodes, f32[8,128]{1,0:T(8,128)S(1)} %get-tuple-element.9._), custom_call_target="tpu_custom_call" | custom-call | tf_op jit(solution)/shard_map/pallas_call | solution.py:808
  47.6 1.1 %shard_map.44 = f32[2,256,1024]{2,1,0:T(8,128)} custom-call(f32[2,160,1024]{2,1,0:T(8,128)S(1)} %shard_map.43.rest, f32[2,256,1024]{2,1,0:T(8,128)} %get-tuple-element.10._), custom_call_target="tpu_custom_call", output_to_operand_aliasing={{}: (1, {})} | custom-call | tf_op jit(solution)/shard_map/pallas_call | solution.py:818

commit v6 on v5

--- a/solution.py
+++ b/solution.py
@@ -493,6 +493,17 @@
         def _(step):
             coarse_compute(step)
 
+    greets_first = low_row // slab > 1
+    other_rank = jnp.logical_not(coarse_rank)
+
+    if greets_first:
+
+        @pl.when(other_rank)
+        def _():
+            greet()
+            answered()
+            halo_exchange((0, 1), False)
+
     strips = columns // LANES // PARTS
 
     def step_at(index):
@@ -565,14 +576,13 @@
                     def _():
                         strip_compute(block, pl.multiple_of(low, LANES), False)
 
-                @pl.when(jnp.logical_not(coarse_rank) & (step == 0) & (part == 0))
-                def _():
-                    greet()
-
-                @pl.when(jnp.logical_not(coarse_rank) & (step == 0) & (part == 1))
-                def _():
-                    answered()
-                    halo_exchange((0, 1), False)
+                if not greets_first:
+                    pl.when(other_rank & (step == 0) & (part == 0))(greet)
+
+                    @pl.when(other_rank & (step == 0) & (part == 1))
+                    def _():
+                        answered()
+                        halo_exchange((0, 1), False)
 
                 @pl.when((index < early) | (index >= turn))
                 def _():

time: 49.4 us -> 49.4 us (level)
  no operation moved by 1% of the time
where the time goes in v6:
time: 49.4 us; the launch traced here: 48.7 us
  Pallas kernels  48.1 us (97%)
  between operations  0.65 us (1%)
    pallas_call x1, Pallas kernels, body(): pl.pallas_call(kernel, out_shape=(OUT((2, slab, columns), jnp.float32), O...  24.9 us
    pallas_call x1, Pallas kernels, body(): pl.pallas_call(functools.partial(send_rest, coarse_rows), out_shape=OUT((...  19.7 us
    pallas_call x1, Pallas kernels, body(): pl.pallas_call(functools.partial(write_out, coarse_rows), out_shape=(jax....  2.37 us
    pallas_call x1, Pallas kernels, body(): pl.pallas_call(functools.partial(write_rest, coarse_rows), out_shape=jax....  1.06 us

profile of v6, /device:TPU:9, one launch (start us, length us, event | category | flops | bytes accessed | tf_op | source)
XLA Modules:
  0.0 48.7 jit_solution(9704189481921137216)
XLA Ops:
  0.6 24.9 %shard_map.41 = (f32[2,256,1024]{2,1,0:T(8,128)S(1)}, f32[2,2,256,1024]{3,2,1,0:T(8,128)S(1)}) custom-call(f32[2,256,1024]{2,1,0:T(8,128)} %bitcast.5, f32[2,2,256,1024]{3,2,1,0:T(8,128)} %bitcast.4), custom_call_target="tpu_custom_call" | custom-call | tf_op jit(solution)/shard_map/pallas_call | solution.py:776
  25.5 2.4 %shard_map.42 = (f32[2,256,1024]{2,1,0:T(8,128)}, f32[2,2,256,1024]{3,2,1,0:T(8,128)}, f32[8,128]{1,0:T(8,128)S(1)}) custom-call(f32[2,256,1024]{2,1,0:T(8,128)S(1)} %get-tuple-element.8.start, f32[2,2,256,1024]{3,2,1,0:T(8,128)S(1)} %get-tuple-element.7.nodes), custom_call_target="tpu_custom_call" | custom-call | tf_op jit(solution)/shard_map/pallas_call | solution.py:805
  27.9 19.7 %shard_map.43.rest = f32[2,160,1024]{2,1,0:T(8,128)S(1)} custom-call(f32[2,2,256,1024]{3,2,1,0:T(8,128)S(1)} %get-tuple-element.7.nodes, f32[8,128]{1,0:T(8,128)S(1)} %get-tuple-element.9._), custom_call_target="tpu_custom_call" | custom-call | tf_op jit(solution)/shard_map/pallas_call | solution.py:818
  47.6 1.1 %shard_map.44 = f32[2,256,1024]{2,1,0:T(8,128)} custom-call(f32[2,160,1024]{2,1,0:T(8,128)S(1)} %shard_map.43.rest, f32[2,256,1024]{2,1,0:T(8,128)} %get-tuple-element.10._), custom_call_target="tpu_custom_call", output_to_operand_aliasing={{}: (1, {})} | custom-call | tf_op jit(solution)/shard_map/pallas_call | solution.py:828

commit v7 on v6

--- a/solution.py
+++ b/solution.py
@@ -115,21 +115,19 @@
 
     side_rows = coarse_rows + inward
     head_rows = BLOCK + 2 * HALO if inward else 0
-    first_rows, width = BLOCK + HALO, columns // PARTS
+    first_rows, width = BLOCK + HALO, columns // 2
     rest_rows = slab - first_rows - BLOCK
 
     def load_first():
         top = jnp.where(lower, slab - side_rows, 0)
         if head_rows:
-            load(3, jnp.where(lower, top, side_rows - head_rows), head_rows, 0, LANES)
+            load(3, jnp.where(lower, top, side_rows - head_rows), head_rows, 0, low_column)
         else:
             load(0, top, side_rows, low_column, CX)
 
     def load_coarse_rank():
         top = jnp.where(lower, slab - side_rows, 0)
         if head_rows:
-            first_top = jnp.where(lower, top, side_rows - head_rows)
-            load(4, first_top, head_rows, LANES, low_column - LANES)
             load(0, top, side_rows, low_column, CX)
         rest = jnp.where(lower, top + head_rows, 0)
         load(1, rest, side_rows - head_rows, 0, low_column)
@@ -141,10 +139,10 @@
         load(part, jnp.where(lower, 0, slab - first_rows), first_rows, part * width, width)
 
     def load_other_rank():
-        pl.loop(1, PARTS)(load_part)
-
-        load(PARTS, jnp.where(lower, first_rows, rest_rows), BLOCK, 0, columns)
-        load(PARTS + 1, jnp.where(lower, slab - rest_rows, 0), rest_rows, 0, columns)
+        load_part(1)
+
+        load(2, jnp.where(lower, first_rows, rest_rows), BLOCK, 0, columns)
+        load(3, jnp.where(lower, slab - rest_rows, 0), rest_rows, 0, columns)
 
     def begin_copies():
         def copy(top, height, left, width):
@@ -333,12 +331,6 @@
             def _(part):
                 bulk(PARTS * step + part)
 
-    pl.when(coarse_rank)(load_first)
-
-    @pl.when(jnp.logical_not(coarse_rank))
-    def _():
-        load_part(0)
-
     barrier = pltpu.get_barrier_semaphore()
     for there, exists in (
         ({"tm": tm - 1}, has_prev),
@@ -348,6 +340,12 @@
         @pl.when(exists)
         def _(there=there):
             pl.semaphore_signal(barrier, inc=1, device_id=there, device_id_type=MESH)
+
+    pl.when(coarse_rank)(load_first)
+
+    @pl.when(jnp.logical_not(coarse_rank))
+    def _():
+        load_part(0)
 
     pl.when(coarse_rank)(load_coarse_rank)
     pl.when(jnp.logical_not(coarse_rank))(load_other_rank)
@@ -467,7 +465,7 @@
     @pl.when(coarse_rank)
     def _():
         if head_rows:
-            loaded(3, head_rows, LANES)
+            loaded(3, head_rows, low_column)
 
             @pl.loop(0, low_column // LANES)
             def _(strip):
@@ -478,10 +476,6 @@
                 @pl.when(has_next)
                 def _():
                     bulk_copy(block_of(0), left, LANES)
-
-                @pl.when(strip == 0)
-                def _():
-                    loaded(4, head_rows, low_column - LANES)
         else:
             greet()
         loaded(0, side_rows, CX)
@@ -547,9 +541,9 @@
                 def _():
                     loaded(2, slab - side_rows, columns)
 
-            for slot, height in ((PARTS, BLOCK), (PARTS + 1, rest_rows)):
-
-                @pl.when(jnp.logical_not(coarse_rank) & (step == slot - PARTS + 1))
+            for slot, height in ((2, BLOCK), (3, rest_rows)):
+
+                @pl.when(jnp.logical_not(coarse_rank) & (step == slot - 1))
                 def _(slot=slot, height=height):
                     loaded(slot, height, columns)
 
@@ -561,9 +555,9 @@
 
             @pl.loop(0, PARTS)
             def _(part):
-                @pl.when(jnp.logical_not(coarse_rank) & (step == 0))
+                @pl.when(jnp.logical_not(coarse_rank) & (step == 0) & (part % (PARTS // 2) == 0))
                 def _():
-                    loaded(part, first_rows, width)
+                    loaded(part // (PARTS // 2), first_rows, width)
 
                 @pl.loop(0, strips)
                 def _(strip):
@@ -785,7 +779,7 @@
             pltpu.VMEM((3, 2, slab + 2 * HALO, columns), jnp.float32),
             pltpu.VMEM((2, coarse_rows, CX), jnp.float32),
             pltpu.VMEM((2, coarse_rows, CX), jnp.float32),
-            dma((PARTS + 2,)),
+            dma((4,)),
             dma((2,)),
             dma((2, 2)),
             dma,

time: 49.4 us -> 49.4 us (level)
  no operation moved by 1% of the time
where the time goes in v7:
time: 49.4 us; the launch traced here: 48.7 us
  Pallas kernels  48 us (97%)
  between operations  0.65 us (1%)
    pallas_call x1, Pallas kernels, body(): pl.pallas_call(kernel, out_shape=(OUT((2, slab, columns), jnp.float32), O...  24.9 us
    pallas_call x1, Pallas kernels, body(): pl.pallas_call(functools.partial(send_rest, coarse_rows), out_shape=OUT((...  19.7 us
    pallas_call x1, Pallas kernels, body(): pl.pallas_call(functools.partial(write_out, coarse_rows), out_shape=(jax....  2.37 us
    pallas_call x1, Pallas kernels, body(): pl.pallas_call(functools.partial(write_rest, coarse_rows), out_shape=jax....  1.06 us

profile of v7, /device:TPU:9, one launch (start us, length us, event | category | flops | bytes accessed | tf_op | source)
XLA Modules:
  0.0 48.7 jit_solution(7573326255261334220)
XLA Ops:
  0.6 24.9 %shard_map.41 = (f32[2,256,1024]{2,1,0:T(8,128)S(1)}, f32[2,2,256,1024]{3,2,1,0:T(8,128)S(1)}) custom-call(f32[2,256,1024]{2,1,0:T(8,128)} %bitcast.5, f32[2,2,256,1024]{3,2,1,0:T(8,128)} %bitcast.4), custom_call_target="tpu_custom_call" | custom-call | tf_op jit(solution)/shard_map/pallas_call | solution.py:770
  25.5 2.4 %shard_map.42 = (f32[2,256,1024]{2,1,0:T(8,128)}, f32[2,2,256,1024]{3,2,1,0:T(8,128)}, f32[8,128]{1,0:T(8,128)S(1)}) custom-call(f32[2,256,1024]{2,1,0:T(8,128)S(1)} %get-tuple-element.8.start, f32[2,2,256,1024]{3,2,1,0:T(8,128)S(1)} %get-tuple-element.7.nodes), custom_call_target="tpu_custom_call" | custom-call | tf_op jit(solution)/shard_map/pallas_call | solution.py:799
  27.9 19.7 %shard_map.43.rest = f32[2,160,1024]{2,1,0:T(8,128)S(1)} custom-call(f32[2,2,256,1024]{3,2,1,0:T(8,128)S(1)} %get-tuple-element.7.nodes, f32[8,128]{1,0:T(8,128)S(1)} %get-tuple-element.9._), custom_call_target="tpu_custom_call" | custom-call | tf_op jit(solution)/shard_map/pallas_call | solution.py:812
  47.6 1.1 %shard_map.44 = f32[2,256,1024]{2,1,0:T(8,128)} custom-call(f32[2,160,1024]{2,1,0:T(8,128)S(1)} %shard_map.43.rest, f32[2,256,1024]{2,1,0:T(8,128)} %get-tuple-element.10._), custom_call_target="tpu_custom_call", output_to_operand_aliasing={{}: (1, {})} | custom-call | tf_op jit(solution)/shard_map/pallas_call | solution.py:822

commit v8 on v7

--- a/solution.py
+++ b/solution.py
@@ -23,7 +23,7 @@
 DEFER = 5
 WRITES = 2
 DETOURS = 3
-DETOUR_ROWS = 16
+DETOUR_ROWS = 24
 TURN = 2
 EARLY = 3
 PIECES = 4
@@ -45,7 +45,7 @@
 
 
 def defers(tm, slab, coarse_rows):
-    return tm < DEFER if slab > coarse_rows else tm < 0
+    return (tm < DEFER) & (tm > 0) if slab > coarse_rows else tm < 0
 
 
 def kernel(
@@ -460,7 +460,7 @@
 
     never = blocks + 1
     turn = jnp.where(coarse_rank, jnp.minimum(TURN * tm, blocks), never)
-    early = jnp.where(coarse_rank, jnp.where(deferred(tm), jnp.minimum(EARLY * tm // 4, turn), turn), blocks)
+    early = jnp.where(coarse_rank, jnp.where(tm < DEFER, jnp.minimum(EARLY * tm // 4, turn), turn), blocks)
 
     @pl.when(coarse_rank)
     def _():

time: 49.4 us -> 49.4 us (level)
  no operation moved by 1% of the time
where the time goes in v8:
time: 49.4 us; the launch traced here: 48.5 us
  Pallas kernels  47.9 us (97%)
  between operations  0.65 us (1%)
    pallas_call x1, Pallas kernels, body(): pl.pallas_call(kernel, out_shape=(OUT((2, slab, columns), jnp.float32), O...  24.9 us
    pallas_call x1, Pallas kernels, body(): pl.pallas_call(functools.partial(send_rest, coarse_rows), out_shape=OUT((...  19.6 us
    pallas_call x1, Pallas kernels, body(): pl.pallas_call(functools.partial(write_out, coarse_rows), out_shape=(jax....  2.37 us
    pallas_call x1, Pallas kernels, body(): pl.pallas_call(functools.partial(write_rest, coarse_rows), out_shape=jax....  1.06 us

profile of v8, /device:TPU:9, one launch (start us, length us, event | category | flops | bytes accessed | tf_op | source)
XLA Modules:
  0.0 48.5 jit_solution(8015500171610245950)
XLA Ops:
  0.6 24.9 %shard_map.41 = (f32[2,256,1024]{2,1,0:T(8,128)S(1)}, f32[2,2,256,1024]{3,2,1,0:T(8,128)S(1)}) custom-call(f32[2,256,1024]{2,1,0:T(8,128)} %bitcast.5, f32[2,2,256,1024]{3,2,1,0:T(8,128)} %bitcast.4), custom_call_target="tpu_custom_call" | custom-call | tf_op jit(solution)/shard_map/pallas_call | solution.py:770
  25.5 2.4 %shard_map.42 = (f32[2,256,1024]{2,1,0:T(8,128)}, f32[2,2,256,1024]{3,2,1,0:T(8,128)}, f32[8,128]{1,0:T(8,128)S(1)}) custom-call(f32[2,256,1024]{2,1,0:T(8,128)S(1)} %get-tuple-element.8.start, f32[2,2,256,1024]{3,2,1,0:T(8,128)S(1)} %get-tuple-element.7.nodes), custom_call_target="tpu_custom_call" | custom-call | tf_op jit(solution)/shard_map/pallas_call | solution.py:799
  27.9 19.6 %shard_map.43.rest = f32[2,160,1024]{2,1,0:T(8,128)S(1)} custom-call(f32[2,2,256,1024]{3,2,1,0:T(8,128)S(1)} %get-tuple-element.7.nodes, f32[8,128]{1,0:T(8,128)S(1)} %get-tuple-element.9._), custom_call_target="tpu_custom_call" | custom-call | tf_op jit(solution)/shard_map/pallas_call | solution.py:812
  47.5 1.1 %shard_map.44 = f32[2,256,1024]{2,1,0:T(8,128)} custom-call(f32[2,160,1024]{2,1,0:T(8,128)S(1)} %shard_map.43.rest, f32[2,256,1024]{2,1,0:T(8,128)} %get-tuple-element.10._), custom_call_target="tpu_custom_call", output_to_operand_aliasing={{}: (1, {})} | custom-call | tf_op jit(solution)/shard_map/pallas_call | solution.py:822
